TPU v7x, 128 devices: a whole 4x4x4 slice. The times are simulated.
128 devices in a mesh: pts: 32 (over z, y_hi, x), orb: 4 (over y_lo, core).
Axes of the slice: x: 4, y: 4 (y_hi: 2, y_lo: 2; y = y_hi * 2 + y_lo), z: 4, core: 2. Of those that a mesh axis runs over, the one named last changes fastest.
Arguments:
- occ_points: float32 [20480, 1024], P('pts', 'orb'), may hold values from -0.1875 to 0.1875
- vir_points: float32 [20480, 9216], P('pts', 'orb'), may hold values from -0.0625 to 0.0625
- occ_cols: float32 [256, 1024], P('pts', 'orb'), may hold values from -6 to 6
- vir_cols: float32 [256, 9216], P('pts', 'orb'), may hold values from -6 to 6
- occ_energy: float32 [1024], P('orb'), may hold values from -1.5 to -0.2
- vir_energy: float32 [9216], P('orb'), may hold values from 0.2 to 3
- plane_waves: float32 [8192, 20480], P('orb', 'pts'), may hold values from -0.0390625 to 0.0390625
Outputs:
- projected: float32 [2, 8192, 256], P(None, 'orb', 'pts')
All inputs are finite; a program needn't handle non-finite values.
Results may differ from a plain program's by a relative error of at most 0.00011.
Values sent between devices are 32-bit elements; how exact they have to be, the bound alone decides.
No kernel may reach another device: no remote copies, remote signals or barrier semaphores. Data moves between devices by JAX's collectives and lax.ppermute only.
A program may use at most 64 MiB of HBM per device.

v0:
```python
import math

import jax
import jax.numpy as jnp
from jax import lax
from jax.experimental import pallas as pl
from jax.experimental.pallas import tpu as pltpu
from jax.sharding import Mesh
from jax.sharding import PartitionSpec as P

PTS = ("z", "yh", "x")
ORB = ("yl", "core")
SIDE = 4

IMAG_TIMES = (0.3, 1.2)
FREQUENCIES = (0.5, 2.0)
QUAD_WEIGHTS = (0.6, 1.8)
TABLE = [[2.0 * q * math.cos(w * t) for q, t in zip(QUAD_WEIGHTS, IMAG_TIMES)] for w in FREQUENCIES]

MIB = 1024 * 1024


def limit(mib):
    return pltpu.CompilerParams(vmem_limit_bytes=mib * MIB)


def swap(x, axis):
    return lax.ppermute(x, axis, [(0, 1), (1, 0)])


def outer_shift(x, by):
    pairs = []
    for z in range(SIDE):
        for k in range(SIDE):
            for core in range(2):
                to = (z, (k + by) % SIDE) if core else ((z + by) % SIDE, k)
                pairs.append(((z * SIDE + k) * 2 + core, (to[0] * SIDE + to[1]) * 2 + core))
    return lax.ppermute(x, ("z", "x", "core"), pairs)


def inner_shift(x, by):
    pairs = []
    for z in range(SIDE):
        for k in range(SIDE):
            for core in range(2):
                to = ((z + by) % SIDE, k) if core else (z, (k + by) % SIDE)
                pairs.append(((z * SIDE + k) * 2 + core, (to[0] * SIDE + to[1]) * 2 + core))
    return lax.ppermute(x, ("z", "x", "core"), pairs)


def inner_pairs(by, other):
    place = lambda z, y, x, c: (((z % SIDE) * 2 + y) * SIDE + x % SIDE) * 2 + c
    pairs = []
    for z in range(SIDE):
        for y in range(2):
            for x in range(SIDE):
                near = place(z, y, x + by, 1 if other else 0)
                far = place(z + by, 1 - y, x, 0 if other else 1)
                pairs += [(place(z, y, x, 0), near), (place(z, y, x, 1), far)]
    return pairs


def to_owner(x, by, other):
    return lax.ppermute(x, PTS + ("core",), inner_pairs(by, other))


def from_owner(x, by, other):
    pairs = [(b, a) for a, b in inner_pairs(by, other)]
    return lax.ppermute(x, PTS + ("core",), pairs)


def joined(blocks, axis):
    shape = list(blocks[0].shape)
    shape[axis] = sum(b.shape[axis] for b in blocks)

    def body(*refs):
        start = 0
        for r in refs[:-1]:
            at = pl.ds(start, r.shape[axis])
            if axis:
                refs[-1][:, at] = r[...]
            else:
                refs[-1][at, :] = r[...]
            start += r.shape[axis]

    return pl.pallas_call(
        body,
        out_shape=jax.ShapeDtypeStruct(tuple(shape), blocks[0].dtype),
        compiler_params=limit(6),
        name="joined",
    )(*blocks)


def picked(blocks, energy, occ_count, core_width):
    rows = blocks[0].shape[0]
    n = len(blocks)

    def body(*refs):
        ins, last, out = refs[: 2 * n], refs[2 * n], refs[2 * n + 1]
        for i in range(n):
            for s in range(2):
                at = (pl.ds(i * rows, rows), pl.ds(s * occ_count, occ_count))
                out[at] = ins[2 * i + s][...]
        out[pl.ds(n * rows, 8), :] = last[...]

    def slot(s):
        at = s * core_width // occ_count
        return pl.BlockSpec((rows, occ_count), lambda i: (0, at))

    return pl.pallas_call(
        body,
        grid=(1,),
        in_specs=[slot(s) for _ in range(n) for s in range(2)]
        + [pl.BlockSpec(energy.shape, lambda i: (0, 0))],
        out_specs=pl.BlockSpec((n * rows + 8, 2 * occ_count), lambda i: (0, 0)),
        out_shape=jax.ShapeDtypeStruct((n * rows + 8, 2 * occ_count), blocks[0].dtype),
        compiler_params=limit(4),
        name="picked",
    )(*[b for b in blocks for _ in range(2)], energy)


def parts(x):
    high = x.astype(jnp.bfloat16)
    return high, (x - high.astype(jnp.float32)).astype(jnp.bfloat16)


def contract(left, right):
    return lax.dot_general(
        left, right, (((1,), (1,)), ((), ())), preferred_element_type=jnp.float32
    )


def contract_parts(stacked, right):
    rows = stacked.shape[0] // 2
    high, low = parts(right)
    both = contract(stacked, high)
    return (both[:rows] + both[rows:]) + contract(stacked[:rows], low)


def vir_greens(blocks, weight, point_sets, occ_count):
    n = len(blocks)
    rows = blocks[0].shape[0]
    half = blocks[0].shape[1] // 2
    width = half - occ_count
    points = point_sets[0].shape[0]
    step = 768 if width % 768 == 0 else width
    per = width // step
    total = 2 * n * rows

    def body(*refs):
        ins, w_ref = refs[:n], refs[n]
        sets = refs[n + 1 : n + 3]
        out, stacked = refs[n + 3 :]
        i = pl.program_id(0)

        @pl.when(i == 0)
        def _():
            out[...] = jnp.zeros_like(out)

        for s in range(2):

            @pl.when(i // per == s)
            def _(s=s):
                k = pl.multiple_of((i - s * per) * step, 128)
                w = w_ref[:, pl.ds(s * width + k, step)]
                for j in range(n):
                    x = ins[j][:, pl.ds(s * half + occ_count + k, step)]
                    for t in range(2):
                        at = (t * n + j) * rows
                        high, low = parts(x * w[t : t + 1])
                        stacked[pl.ds(at, rows), :] = high
                        stacked[pl.ds(total + at, rows), :] = low
                out[...] += contract_parts(stacked[...], sets[s][...])

    whole = lambda a: pl.BlockSpec(a.shape, lambda i: (0, 0))
    return pl.pallas_call(
        body,
        grid=(2 * per,),
        in_specs=[whole(b) for b in blocks]
        + [whole(weight)]
        + [
            pl.BlockSpec((points, step), lambda i: (0, jnp.minimum(i, per - 1))),
            pl.BlockSpec((points, step), lambda i: (0, jnp.maximum(i - per, 0))),
        ],
        out_specs=pl.BlockSpec((total, points), lambda i: (0, 0)),
        out_shape=jax.ShapeDtypeStruct((total, points), jnp.float32),
        scratch_shapes=[pltpu.VMEM((2 * total, step), jnp.bfloat16)],
        compiler_params=limit(24),
        cost_estimate=pl.CostEstimate(
            flops=6 * total * points * 2 * width, bytes_accessed=14_000_000, transcendentals=0
        ),
        name="vir_greens",
    )(*blocks, weight, *point_sets)


def occ_greens(here, there, point_sets):
    columns = here.shape[0] - 8
    width = here.shape[1]
    points, count = point_sets[0].shape

    def body(here_ref, there_ref, *refs):
        sets, (out, stacked) = refs[:4], refs[4:]
        total = None
        for chip, ref in enumerate((here_ref, there_ref)):
            energy = ref[pl.ds(columns, 1), :]
            for t in range(2):
                x = ref[pl.ds(0, columns), :] * jnp.exp(IMAG_TIMES[t] * energy)
                high, low = parts(x)
                k = pl.ds(chip * width, width)
                stacked[pl.ds(t * columns, columns), k] = high
                stacked[pl.ds((2 + t) * columns, columns), k] = low
        for i in range(4):
            part = contract_parts(stacked[:, pl.ds(i * count, count)], sets[i][...])
            total = part if total is None else total + part
        out[...] = total

    return pl.pallas_call(
        body,
        out_shape=jax.ShapeDtypeStruct((2 * columns, points), jnp.float32),
        scratch_shapes=[pltpu.VMEM((4 * columns, 2 * width), jnp.bfloat16)],
        compiler_params=limit(16),
        name="occ_greens",
    )(here, there, *point_sets)


def projections(vir_here, vir_there, occ, wave_sets, own):
    rows, points = occ.shape
    waves = wave_sets[0].shape[0]
    step = 512
    per = waves // step
    blocks = rows // (2 * own * SIDE)
    share = rows // blocks
    inner = share // (2 * own)

    def body(a_ref, b_ref, o_ref, w_first, w_last, *refs):
        outs, stacked = refs[:-1], refs[-1]
        i = pl.program_id(0)

        @pl.when(i == 0)
        def _():
            response = -(o_ref[...] * (a_ref[...] + b_ref[...]))
            early, late = response[: rows // 2], response[rows // 2 :]
            spectral = [TABLE[k][0] * early + TABLE[k][1] * late for k in range(2)]
            for j in range(blocks * inner):
                both = jnp.concatenate([s[j * own : (j + 1) * own] for s in spectral], axis=0)
                high, low = parts(both)
                stacked[pl.ds(2 * own * j, 2 * own), :] = high
                stacked[pl.ds(rows + 2 * own * j, 2 * own), :] = low

        for s, w_ref in enumerate((w_first, w_last)):

            @pl.when(i // per == s)
            def _(s=s, w_ref=w_ref):
                result = contract_parts(stacked[...], w_ref[...])
                for d in range(blocks):
                    outs[s * blocks + d][...] = result[d * share : (d + 1) * share]

    whole = pl.BlockSpec((rows, points), lambda i: (0, 0))
    first = lambda i: jnp.minimum(i, per - 1)
    last = lambda i: jnp.maximum(i - per, 0)
    return pl.pallas_call(
        body,
        grid=(2 * per,),
        in_specs=[whole] * 3
        + [
            pl.BlockSpec((step, points), lambda i: (first(i), 0)),
            pl.BlockSpec((step, points), lambda i: (last(i), 0)),
        ],
        out_specs=[pl.BlockSpec((share, step), lambda i: (0, first(i)))] * blocks
        + [pl.BlockSpec((share, step), lambda i: (0, last(i)))] * blocks,
        out_shape=[jax.ShapeDtypeStruct((share, waves), jnp.float32)] * (2 * blocks),
        scratch_shapes=[pltpu.VMEM((2 * rows, points), jnp.bfloat16)],
        compiler_params=limit(24),
        cost_estimate=pl.CostEstimate(
            flops=12 * rows * points * waves, bytes_accessed=14_000_000, transcendentals=0
        ),
        name="projections",
    )(vir_here, vir_there, occ, *wave_sets)


def summed_blocks(arrays):
    rows, waves = arrays[0].shape
    step = 1024
    share = rows // SIDE

    def body(*refs):
        total = refs[0][...]
        for r in refs[1:SIDE]:
            total = total + r[...]
        for d in range(SIDE):
            refs[SIDE + d][...] = total[d * share : (d + 1) * share]

    return pl.pallas_call(
        body,
        grid=(waves // step,),
        in_specs=[pl.BlockSpec((rows, step), lambda i: (0, i))] * SIDE,
        out_specs=[pl.BlockSpec((share, step), lambda i: (0, i))] * SIDE,
        out_shape=[jax.ShapeDtypeStruct((share, waves), jnp.float32)] * SIDE,
        compiler_params=limit(12),
        cost_estimate=pl.CostEstimate(
            flops=3 * rows * waves, bytes_accessed=20 * rows * waves, transcendentals=0
        ),
        name="summed_blocks",
    )(*arrays)


def after(x, event):
    return lax.optimization_barrier((x, event))[0]


def on_device(occ_points, vir_points, occ_cols, vir_cols, occ_energy, vir_energy, plane_waves):
    _, occ_count = occ_points.shape
    own = occ_cols.shape[0]
    moments = jnp.array(IMAG_TIMES, jnp.float32)

    cols = joined([occ_cols, vir_cols], 1)
    block = joined([from_owner(cols, 0, other) for other in (False, True)], 1)
    occ_points_there = swap(after(occ_points, block), "yl")
    block = joined([block] + [inner_shift(block, -d) for d in range(1, SIDE)], 0)
    blocks = [block] + [None] * (SIDE - 1)
    for d in (1, 3, 2):
        blocks[d] = outer_shift(block, -d)

    energy = jnp.concatenate([occ_energy, vir_energy])
    energy_other = swap(energy, "core")
    vir_both = jnp.concatenate([vir_energy, energy_other[occ_count:]])
    vir_weight = jnp.exp(-moments[:, None] * vir_both[None, :])
    occ_chip = jnp.concatenate([occ_energy, energy_other[:occ_count]])
    occ_chip = jnp.broadcast_to(occ_chip[None], (8, 2 * occ_count))
    vir_sets = (vir_points, swap(vir_points, "core"))
    occ_sets = None

    sums = [[None] * SIDE for _ in range(2)]
    for group in ((1, 3), (0, 2)):
        pair = [blocks[d] for d in group]
        occ_here = picked(pair, occ_chip, occ_count, cols.shape[1])
        occ_there = swap(occ_here, "yl")
        vir_here = vir_greens(pair, vir_weight, vir_sets, occ_count)
        vir_there = swap(vir_here, "yl")
        if occ_sets is None:
            near, far, waves = after((occ_points, occ_points_there, plane_waves), vir_here)
            occ_sets = (near, swap(near, "core"), far, swap(far, "core"))
            wave_sets = (plane_waves, swap(waves, "core"))
        occ_green = occ_greens(occ_here, occ_there, occ_sets)
        found = projections(vir_here, vir_there, occ_green, wave_sets, own)
        for s in range(2):
            for j, d in enumerate(group):
                sums[s][d] = outer_shift(found[2 * s + j], d) if d else found[2 * s + j]

    results = []
    for s, other in enumerate((False, True)):
        finished = summed_blocks(sums[s])
        results += [to_owner(finished[d], d, other) for d in range(SIDE)]
    total = sum(results[1:], results[0])
    return jnp.transpose(total.reshape(2, own, -1), (0, 2, 1))


def solution(mesh):
    split = Mesh(mesh.devices.reshape(SIDE, 2, SIDE, 2, 2), PTS + ORB)
    in_specs = (
        P(PTS, ORB),
        P(PTS, ORB),
        P(PTS, ORB),
        P(PTS, ORB),
        P(ORB),
        P(ORB),
        P(ORB, PTS),
    )
    out_specs = P(None, ORB, PTS)
    return jax.shard_map(
        on_device, mesh=split, in_specs=in_specs, out_specs=out_specs, check_vma=False
    )
```

profile of v0, /device:TPU:1, one launch (start us, length us, event | category | flops | bytes accessed | tf_op | source)
XLA Modules:
  0.0 120.9 jit_solution(9022528907524201134)
XLA Ops:
  0.0 1.4 %collective-permute-start.7 = (f32[640,2304]{1,0:T(8,128)}, f32[640,2304]{1,0:T(8,128)S(1)}, u32[]{:S(2)}, u32[]{:S(2)}) collective-permute-start(f32[640,2304]{1,0:T(8,128)} %refs_3_.3), channel_id=1, source_target_pairs={{0,1},{1,0},{2,3},{3,2},{4,5},{5,4},{6,7},{7,6},{8,9},{9,8},{10,11... | collective-permute-start | bytes 17694728 | tf_op jit(solution)/shard_map/ppermute | solution.py:28
  3.0 4.9 %collective-permute-start = (f32[8,2560]{1,0:T(8,128)S(1)}, f32[8,2560]{1,0:T(8,128)S(1)}, u32[]{:S(2)}, u32[]{:S(2)}) collective-permute-start(f32[8,2560]{1,0:T(8,128)S(1)} %joined.3), channel_id=1, source_target_pairs={{0,0},{17,1},{4,4},{21,5},{8,8},{25,9},{12,12},{29,13},{16,16},{1,... | collective-permute-start | bytes 245768 | tf_op jit(solution)/shard_map/ppermute | solution.py:69
  7.9 3.0 %collective-permute-done.1.refs_1_ = f32[8,2560]{1,0:T(8,128)S(1)} collective-permute-done((f32[8,2560]{1,0:T(8,128)S(1)}, f32[8,2560]{1,0:T(8,128)S(1)}, u32[]{:S(2)}, u32[]{:S(2)}) %collective-permute-start.1) | collective-permute-done | bytes 81952 | tf_op jit(solution)/shard_map/ppermute | solution.py:69
  11.0 1.8 %collective-permute-start.4 = (f32[8,5120]{1,0:T(8,128)S(1)}, f32[8,5120]{1,0:T(8,128)S(1)}, u32[]{:S(2)}, u32[]{:S(2)}) collective-permute-start(f32[8,5120]{1,0:T(8,128)S(1)} %joined.4.refs_0_), channel_id=1, source_target_pairs={{0,4},{1,33},{4,8},{5,37},{8,12},{9,41},{12,0},{13,45},{32,36},{33... | collective-permute-start | bytes 491528 | tf_op jit(solution)/shard_map/ppermute | solution.py:48
  12.8 3.3 %collective-permute-start.3 = (f32[8,5120]{1,0:T(8,128)S(1)}, f32[8,5120]{1,0:T(8,128)S(1)}, u32[]{:S(2)}, u32[]{:S(2)}) collective-permute-start(f32[8,5120]{1,0:T(8,128)S(1)} %joined.4.refs_0_), channel_id=1, source_target_pairs={{0,8},{1,65},{4,12},{5,69},{8,0},{9,73},{12,4},{13,77},{32,40},{33... | collective-permute-start | bytes 491528 | tf_op jit(solution)/shard_map/ppermute | solution.py:48
  19.4 1.3 %collective-permute-start.10 = (f32[640,256]{1,0:T(8,128)}, f32[640,256]{1,0:T(8,128)S(1)}, u32[]{:S(2)}, u32[]{:S(2)}) collective-permute-start(f32[640,256]{1,0:T(8,128)} %refs_0_.3), channel_id=1, source_target_pairs={{0,2},{2,0},{1,3},{3,1},{4,6},{6,4},{5,7},{7,5},{8,10},{10,8},{9,1... | collective-permute-start | bytes 1966088 | tf_op jit(solution)/shard_map/ppermute | solution.py:28
  20.8 1.3 %collective-permute-start.12 = (f32[32,5120]{1,0:T(8,128)S(1)}, f32[32,5120]{1,0:T(8,128)S(1)}, u32[]{:S(2)}, u32[]{:S(2)}) collective-permute-start(f32[32,5120]{1,0:T(8,128)S(1)} %joined.5.refs_0_.refs_1_), channel_id=1, source_target_pairs={{0,32},{1,5},{4,36},{5,9},{8,40},{9,13},{12,44},{13,1},{32,64},{33... | collective-permute-start | bytes 1966088 | tf_op jit(solution)/shard_map/ppermute | solution.py:38
  22.1 1.5 %collective-permute-start.11 = (f32[32,5120]{1,0:T(8,128)S(1)}, f32[32,5120]{1,0:T(8,128)S(1)}, u32[]{:S(2)}, u32[]{:S(2)}) collective-permute-start(f32[32,5120]{1,0:T(8,128)S(1)} %joined.5.refs_0_.refs_1_), channel_id=1, source_target_pairs={{0,96},{1,13},{4,100},{5,1},{8,104},{9,5},{12,108},{13,9},{32,0},{... | collective-permute-start | bytes 1966088 | tf_op jit(solution)/shard_map/ppermute | solution.py:38
  24.3 7.5 %collective-permute-done.12.refs_1_.refs_2_.refs_3_ = f32[32,5120]{1,0:T(8,128)S(1)} collective-permute-done((f32[32,5120]{1,0:T(8,128)S(1)}, f32[32,5120]{1,0:T(8,128)S(1)}, u32[]{:S(2)}, u32[]{:S(2)}) %collective-permute-start.12) | collective-permute-done | bytes 655392 | tf_op jit(solution)/shard_map/ppermute | solution.py:38
  31.8 2.7 %copy-done = f32[640,2304]{1,0:T(8,128)S(1)} copy-done((f32[640,2304]{1,0:T(8,128)S(1)}, f32[640,2304]{1,0:T(8,128)}, u32[]{:S(2)}) %copy-start) | copy-done | bytes 5898264
  34.5 5.7 %vir_greens.3.a_ref = f32[128,640]{1,0:T(8,128)S(1)} custom-call(f32[32,5120]{1,0:T(8,128)S(1)} %collective-permute-done.11.refs_0_.refs_1_, f32[32,5120]{1,0:T(8,128)S(1)} %collective-permute-done.12.refs_1_.refs_2_.refs_3_, f32[2,4608]{1,0:T(2,128)S(1)} %multiply_exponential_fusion.refs_2_, f32[640,2304]{1,0:T(8,128)S(1)} %copy-done, ...), custom_call_target="tpu_custom_call" | custom-call | flops 2264924160 | bytes 14000000 | tf_op jit(solution)/shard_map/vir_greens/pallas_call | solution.py:176
  40.2 2.4 %collective-permute-start.15 = (f32[2048,640]{1,0:T(8,128)S(1)}, f32[2048,640]{1,0:T(8,128)S(1)}, u32[]{:S(2)}, u32[]{:S(2)}) collective-permute-start(f32[2048,640]{1,0:T(8,128)S(1)} %copy-done.2), channel_id=1, source_target_pairs={{0,1},{1,0},{2,3},{3,2},{4,5},{5,4},{6,7},{7,6},{8,9},{9,8},{10,11... | collective-permute-start | bytes 15728648 | tf_op jit(solution)/shard_map/ppermute | solution.py:28
  42.6 2.1 %collective-permute-start.5 = (f32[32,5120]{1,0:T(8,128)S(1)}, f32[32,5120]{1,0:T(8,128)S(1)}, u32[]{:S(2)}, u32[]{:S(2)}) collective-permute-start(f32[32,5120]{1,0:T(8,128)S(1)} %joined.5.refs_0_.refs_1_), channel_id=1, source_target_pairs={{0,64},{1,9},{4,68},{5,13},{8,72},{9,1},{12,76},{13,5},{32,96},{33... | collective-permute-start | bytes 1966088 | tf_op jit(solution)/shard_map/ppermute | solution.py:38
  44.7 1.5 %collective-permute-start.13 = (f32[640,256]{1,0:T(8,128)S(1)}, f32[640,256]{1,0:T(8,128)S(1)}, u32[]{:S(2)}, u32[]{:S(2)}) collective-permute-start(f32[640,256]{1,0:T(8,128)S(1)} %copy-done.3), channel_id=1, source_target_pairs={{0,1},{1,0},{2,3},{3,2},{4,5},{5,4},{6,7},{7,6},{8,9},{9,8},{10,11... | collective-permute-start | bytes 1966088 | tf_op jit(solution)/shard_map/ppermute | solution.py:28
  47.2 6.6 %collective-permute-done.5.refs_1_.refs_2_.refs_3_ = f32[32,5120]{1,0:T(8,128)S(1)} collective-permute-done((f32[32,5120]{1,0:T(8,128)S(1)}, f32[32,5120]{1,0:T(8,128)S(1)}, u32[]{:S(2)}, u32[]{:S(2)}) %collective-permute-start.5) | collective-permute-done | bytes 655392 | tf_op jit(solution)/shard_map/ppermute | solution.py:38
  53.8 1.0 collective-permute-start.17
  54.8 5.7 %vir_greens.2.a_ref = f32[128,640]{1,0:T(8,128)S(1)} custom-call(f32[32,5120]{1,0:T(8,128)S(1)} %joined.5.refs_0_.refs_1_, f32[32,5120]{1,0:T(8,128)S(1)} %collective-permute-done.5.refs_1_.refs_2_.refs_3_, f32[2,4608]{1,0:T(2,128)S(1)} %multiply_exponential_fusion.refs_2_, f32[640,2304]{1,0:T(8,128)S(1)} %copy-done.1, ...), custom_call_target="tpu_custom_call" | custom-call | flops 2264924160 | bytes 14000000 | tf_op jit(solution)/shard_map/vir_greens/pallas_call | solution.py:176
  62.0 5.3 %projections.3 = (f32[64,2048]{1,0:T(8,128)S(1)}, f32[64,2048]{1,0:T(8,128)S(1)}, f32[64,2048]{1,0:T(8,128)S(1)}, f32[64,2048]{1,0:T(8,128)S(1)}) custom-call(f32[128,640]{1,0:T(8,128)S(1)} %vir_greens.3.a_ref, f32[128,640]{1,0:T(8,128)S(1)} %collective-permute-done.16.b_ref, f32[128,640]{1,0:T(8,128)S(1)} %occ_greens.3.o_ref, f32[2048,640]{1,0:T(8,128)S(1)} %copy-done.2, ...), custom_call_target="tpu_custom_call" | custom-call | flops 2013265920 | bytes 14000000 | tf_op jit(solution)/shard_map/projections/pallas_call | solution.py:261
  67.4 1.1 collective-permute-start.18
  68.5 1.4 %collective-permute-start.9 = (f32[72,512]{1,0:T(8,128)S(1)}, f32[72,512]{1,0:T(8,128)S(1)}, u32[]{:S(2)}, u32[]{:S(2)}) collective-permute-start(f32[72,512]{1,0:T(8,128)S(1)} %picked.2.here_ref), channel_id=1, source_target_pairs={{0,2},{2,0},{1,3},{3,1},{4,6},{6,4},{5,7},{7,5},{8,10},{10,8},{9,1... | collective-permute-start | bytes 442376 | tf_op jit(solution)/shard_map/ppermute | solution.py:28
  69.9 2.7 %collective-permute-done.9.there_ref = f32[72,512]{1,0:T(8,128)S(1)} collective-permute-done((f32[72,512]{1,0:T(8,128)S(1)}, f32[72,512]{1,0:T(8,128)S(1)}, u32[]{:S(2)}, u32[]{:S(2)}) %collective-permute-start.9) | collective-permute-done | bytes 147488 | tf_op jit(solution)/shard_map/ppermute | solution.py:28
  73.5 1.9 %collective-permute-start.20 = (f32[64,2048]{1,0:T(8,128)S(1)}, f32[64,2048]{1,0:T(8,128)S(1)}, u32[]{:S(2)}, u32[]{:S(2)}) collective-permute-start(f32[64,2048]{1,0:T(8,128)S(1)} %get-tuple-element.32), channel_id=1, source_target_pairs={{0,96},{1,13},{4,100},{5,1},{8,104},{9,5},{12,108},{13,9},{32,0},{... | collective-permute-start | bytes 1572872 | tf_op jit(solution)/shard_map/ppermute | solution.py:38
  75.4 5.3 %projections.2 = (f32[64,2048]{1,0:T(8,128)S(1)}, f32[64,2048]{1,0:T(8,128)S(1)}, f32[64,2048]{1,0:T(8,128)S(1)}, f32[64,2048]{1,0:T(8,128)S(1)}) custom-call(f32[128,640]{1,0:T(8,128)S(1)} %vir_greens.2.a_ref, f32[128,640]{1,0:T(8,128)S(1)} %collective-permute-done.8.b_ref, f32[128,640]{1,0:T(8,128)S(1)} %occ_greens.2.o_ref, f32[2048,640]{1,0:T(8,128)S(1)} %copy-done.2, ...), custom_call_target="tpu_custom_call" | custom-call | flops 2013265920 | bytes 14000000 | tf_op jit(solution)/shard_map/projections/pallas_call | solution.py:261
  82.2 2.1 %collective-permute-start.27 = (f32[64,2048]{1,0:T(8,128)S(1)}, f32[64,2048]{1,0:T(8,128)S(1)}, u32[]{:S(2)}, u32[]{:S(2)}) collective-permute-start(f32[64,2048]{1,0:T(8,128)S(1)} %get-tuple-element.40), channel_id=1, source_target_pairs={{0,96},{1,13},{4,100},{5,1},{8,104},{9,5},{12,108},{13,9},{32,0},{... | collective-permute-start | bytes 1572872 | tf_op jit(solution)/shard_map/ppermute | solution.py:38
  85.2 5.4 %collective-permute-done.19.refs_2_ = f32[64,2048]{1,0:T(8,128)S(1)} collective-permute-done((f32[64,2048]{1,0:T(8,128)S(1)}, f32[64,2048]{1,0:T(8,128)S(1)}, u32[]{:S(2)}, u32[]{:S(2)}) %collective-permute-start.19) | collective-permute-done | bytes 524320 | tf_op jit(solution)/shard_map/ppermute | solution.py:38
  91.0 4.5 %collective-permute-start.21 = (f32[16,2048]{1,0:T(8,128)S(1)}, f32[16,2048]{1,0:T(8,128)S(1)}, u32[]{:S(2)}, u32[]{:S(2)}) collective-permute-start(f32[16,2048]{1,0:T(8,128)S(1)} %get-tuple-element.33), channel_id=1, source_target_pairs={{0,0},{1,17},{4,4},{5,21},{8,8},{9,25},{12,12},{13,29},{16,16},{17... | collective-permute-start | bytes 393224 | tf_op jit(solution)/shard_map/ppermute | solution.py:64
  95.5 1.4 %collective-permute-start.22 = (f32[16,2048]{1,0:T(8,128)S(1)}, f32[16,2048]{1,0:T(8,128)S(1)}, u32[]{:S(2)}, u32[]{:S(2)}) collective-permute-start(f32[16,2048]{1,0:T(8,128)S(1)} %get-tuple-element.34), channel_id=1, source_target_pairs={{0,4},{1,49},{4,8},{5,53},{8,12},{9,57},{12,0},{13,61},{16,20},{17... | collective-permute-start | bytes 393224 | tf_op jit(solution)/shard_map/ppermute | solution.py:64
  97.0 5.5 %collective-permute-start.23 = (f32[16,2048]{1,0:T(8,128)S(1)}, f32[16,2048]{1,0:T(8,128)S(1)}, u32[]{:S(2)}, u32[]{:S(2)}) collective-permute-start(f32[16,2048]{1,0:T(8,128)S(1)} %get-tuple-element.35), channel_id=1, source_target_pairs={{0,8},{1,81},{4,12},{5,85},{8,0},{9,89},{12,4},{13,93},{16,24},{17... | collective-permute-start | bytes 393224 | tf_op jit(solution)/shard_map/ppermute | solution.py:64
  103.5 9.2 %collective-permute-start.28 = (f32[16,2048]{1,0:T(8,128)S(1)}, f32[16,2048]{1,0:T(8,128)S(1)}, u32[]{:S(2)}, u32[]{:S(2)}) collective-permute-start(f32[16,2048]{1,0:T(8,128)S(1)} %get-tuple-element.41), channel_id=1, source_target_pairs={{0,1},{1,16},{4,5},{5,20},{8,9},{9,24},{12,13},{13,28},{16,17},{17... | collective-permute-start | bytes 393224 | tf_op jit(solution)/shard_map/ppermute | solution.py:64
  112.7 2.4 %collective-permute-start.30 = (f32[16,2048]{1,0:T(8,128)S(1)}, f32[16,2048]{1,0:T(8,128)S(1)}, u32[]{:S(2)}, u32[]{:S(2)}) collective-permute-start(f32[16,2048]{1,0:T(8,128)S(1)} %get-tuple-element.43), channel_id=1, source_target_pairs={{0,9},{1,80},{4,13},{5,84},{8,1},{9,88},{12,5},{13,92},{16,25},{17... | collective-permute-start | bytes 393224 | tf_op jit(solution)/shard_map/ppermute | solution.py:64
  115.1 3.1 %collective-permute-start.31 = (f32[16,2048]{1,0:T(8,128)S(1)}, f32[16,2048]{1,0:T(8,128)S(1)}, u32[]{:S(2)}, u32[]{:S(2)}) collective-permute-start(f32[16,2048]{1,0:T(8,128)S(1)} %get-tuple-element.44), channel_id=1, source_target_pairs={{0,13},{1,112},{4,1},{5,116},{8,5},{9,120},{12,9},{13,124},{16,29}... | collective-permute-start | bytes 393224 | tf_op jit(solution)/shard_map/ppermute | solution.py:64
  118.3 1.6 %collective-permute-done.30 = f32[16,2048]{1,0:T(8,128)S(1)} collective-permute-done((f32[16,2048]{1,0:T(8,128)S(1)}, f32[16,2048]{1,0:T(8,128)S(1)}, u32[]{:S(2)}, u32[]{:S(2)}) %collective-permute-start.30) | collective-permute-done | bytes 131104 | tf_op jit(solution)/shard_map/ppermute | solution.py:64
  (67 shorter events, 14.0 us)
Async XLA Ops:
  0.0 31.8 %collective-permute-start.7 = (f32[640,2304]{1,0:T(8,128)}, f32[640,2304]{1,0:T(8,128)S(1)}, u32[]{:S(2)}, u32[]{:S(2)}) collective-permute-start(f32[640,2304]{1,0:T(8,128)} %refs_3_.3), channel_id=1, source_target_pairs={{0,1},{1,0},{2,3},{3,2},{4,5},{5,4},{6,7},{7,6},{8,9},{9,8},{10,11... | collective-permute-start | bytes 17694728 | tf_op jit(solution)/shard_map/ppermute | solution.py:28
  3.0 8.0 %collective-permute-start.1 = (f32[8,2560]{1,0:T(8,128)S(1)}, f32[8,2560]{1,0:T(8,128)S(1)}, u32[]{:S(2)}, u32[]{:S(2)}) collective-permute-start(f32[8,2560]{1,0:T(8,128)S(1)} %joined.3), channel_id=1, source_target_pairs={{1,0},{16,1},{5,4},{20,5},{9,8},{24,9},{13,12},{28,13},{17,16},{0,... | collective-permute-start | bytes 245768 | tf_op jit(solution)/shard_map/ppermute | solution.py:69
  3.0 8.0 %collective-permute-start = (f32[8,2560]{1,0:T(8,128)S(1)}, f32[8,2560]{1,0:T(8,128)S(1)}, u32[]{:S(2)}, u32[]{:S(2)}) collective-permute-start(f32[8,2560]{1,0:T(8,128)S(1)} %joined.3), channel_id=1, source_target_pairs={{0,0},{17,1},{4,4},{21,5},{8,8},{25,9},{12,12},{29,13},{16,16},{1,... | collective-permute-start | bytes 245768 | tf_op jit(solution)/shard_map/ppermute | solution.py:69
  11.0 9.8 %collective-permute-start.4 = (f32[8,5120]{1,0:T(8,128)S(1)}, f32[8,5120]{1,0:T(8,128)S(1)}, u32[]{:S(2)}, u32[]{:S(2)}) collective-permute-start(f32[8,5120]{1,0:T(8,128)S(1)} %joined.4.refs_0_), channel_id=1, source_target_pairs={{0,4},{1,33},{4,8},{5,37},{8,12},{9,41},{12,0},{13,45},{32,36},{33... | collective-permute-start | bytes 491528 | tf_op jit(solution)/shard_map/ppermute | solution.py:48
  12.8 8.0 %collective-permute-start.3 = (f32[8,5120]{1,0:T(8,128)S(1)}, f32[8,5120]{1,0:T(8,128)S(1)}, u32[]{:S(2)}, u32[]{:S(2)}) collective-permute-start(f32[8,5120]{1,0:T(8,128)S(1)} %joined.4.refs_0_), channel_id=1, source_target_pairs={{0,8},{1,65},{4,12},{5,69},{8,0},{9,73},{12,4},{13,77},{32,40},{33... | collective-permute-start | bytes 491528 | tf_op jit(solution)/shard_map/ppermute | solution.py:48
  16.1 4.7 %collective-permute-start.2 = (f32[8,5120]{1,0:T(8,128)S(1)}, f32[8,5120]{1,0:T(8,128)S(1)}, u32[]{:S(2)}, u32[]{:S(2)}) collective-permute-start(f32[8,5120]{1,0:T(8,128)S(1)} %joined.4.refs_0_), channel_id=1, source_target_pairs={{0,12},{1,97},{4,0},{5,101},{8,4},{9,105},{12,8},{13,109},{32,44},... | collective-permute-start | bytes 491528 | tf_op jit(solution)/shard_map/ppermute | solution.py:48
  17.5 1.2 collective-permute-start.6
  19.4 20.8 %collective-permute-start.10 = (f32[640,256]{1,0:T(8,128)}, f32[640,256]{1,0:T(8,128)S(1)}, u32[]{:S(2)}, u32[]{:S(2)}) collective-permute-start(f32[640,256]{1,0:T(8,128)} %refs_0_.3), channel_id=1, source_target_pairs={{0,2},{2,0},{1,3},{3,1},{4,6},{6,4},{5,7},{7,5},{8,10},{10,8},{9,1... | collective-permute-start | bytes 1966088 | tf_op jit(solution)/shard_map/ppermute | solution.py:28
  20.8 11.0 %collective-permute-start.12 = (f32[32,5120]{1,0:T(8,128)S(1)}, f32[32,5120]{1,0:T(8,128)S(1)}, u32[]{:S(2)}, u32[]{:S(2)}) collective-permute-start(f32[32,5120]{1,0:T(8,128)S(1)} %joined.5.refs_0_.refs_1_), channel_id=1, source_target_pairs={{0,32},{1,5},{4,36},{5,9},{8,40},{9,13},{12,44},{13,1},{32,64},{33... | collective-permute-start | bytes 1966088 | tf_op jit(solution)/shard_map/ppermute | solution.py:38
  22.1 9.7 %collective-permute-start.11 = (f32[32,5120]{1,0:T(8,128)S(1)}, f32[32,5120]{1,0:T(8,128)S(1)}, u32[]{:S(2)}, u32[]{:S(2)}) collective-permute-start(f32[32,5120]{1,0:T(8,128)S(1)} %joined.5.refs_0_.refs_1_), channel_id=1, source_target_pairs={{0,96},{1,13},{4,100},{5,1},{8,104},{9,5},{12,108},{13,9},{32,0},{... | collective-permute-start | bytes 1966088 | tf_op jit(solution)/shard_map/ppermute | solution.py:38
  40.2 21.8 %collective-permute-start.15 = (f32[2048,640]{1,0:T(8,128)S(1)}, f32[2048,640]{1,0:T(8,128)S(1)}, u32[]{:S(2)}, u32[]{:S(2)}) collective-permute-start(f32[2048,640]{1,0:T(8,128)S(1)} %copy-done.2), channel_id=1, source_target_pairs={{0,1},{1,0},{2,3},{3,2},{4,5},{5,4},{6,7},{7,6},{8,9},{9,8},{10,11... | collective-permute-start | bytes 15728648 | tf_op jit(solution)/shard_map/ppermute | solution.py:28
  42.6 11.2 %collective-permute-start.5 = (f32[32,5120]{1,0:T(8,128)S(1)}, f32[32,5120]{1,0:T(8,128)S(1)}, u32[]{:S(2)}, u32[]{:S(2)}) collective-permute-start(f32[32,5120]{1,0:T(8,128)S(1)} %joined.5.refs_0_.refs_1_), channel_id=1, source_target_pairs={{0,64},{1,9},{4,68},{5,13},{8,72},{9,1},{12,76},{13,5},{32,96},{33... | collective-permute-start | bytes 1966088 | tf_op jit(solution)/shard_map/ppermute | solution.py:38
  44.7 16.4 %collective-permute-start.13 = (f32[640,256]{1,0:T(8,128)S(1)}, f32[640,256]{1,0:T(8,128)S(1)}, u32[]{:S(2)}, u32[]{:S(2)}) collective-permute-start(f32[640,256]{1,0:T(8,128)S(1)} %copy-done.3), channel_id=1, source_target_pairs={{0,1},{1,0},{2,3},{3,2},{4,5},{5,4},{6,7},{7,6},{8,9},{9,8},{10,11... | collective-permute-start | bytes 1966088 | tf_op jit(solution)/shard_map/ppermute | solution.py:28
  46.2 14.9 %collective-permute-start.14 = (f32[640,256]{1,0:T(8,128)S(1)}, f32[640,256]{1,0:T(8,128)S(1)}, u32[]{:S(2)}, u32[]{:S(2)}) collective-permute-start(f32[640,256]{1,0:T(8,128)S(1)} %collective-permute-done.10.refs_2_), channel_id=1, source_target_pairs={{0,1},{1,0},{2,3},{3,2},{4,5},{5,4},{6,7},{7,6},{8,9},{9,8},{10,11... | collective-permute-start | bytes 1966088 | tf_op jit(solution)/shard_map/ppermute | solution.py:28
  46.2 15.9 %collective-permute-start.16 = (f32[128,640]{1,0:T(8,128)S(1)}, f32[128,640]{1,0:T(8,128)S(1)}, u32[]{:S(2)}, u32[]{:S(2)}) collective-permute-start(f32[128,640]{1,0:T(8,128)S(1)} %vir_greens.3.a_ref), channel_id=1, source_target_pairs={{0,2},{2,0},{1,3},{3,1},{4,6},{6,4},{5,7},{7,5},{8,10},{10,8},{9,1... | collective-permute-start | bytes 983048 | tf_op jit(solution)/shard_map/ppermute | solution.py:28
  53.8 6.7 %collective-permute-start.17 = (f32[72,512]{1,0:T(8,128)S(1)}, f32[72,512]{1,0:T(8,128)S(1)}, u32[]{:S(2)}, u32[]{:S(2)}) collective-permute-start(f32[72,512]{1,0:T(8,128)S(1)} %picked.3.here_ref), channel_id=1, source_target_pairs={{0,2},{2,0},{1,3},{3,1},{4,6},{6,4},{5,7},{7,5},{8,10},{10,8},{9,1... | collective-permute-start | bytes 442376 | tf_op jit(solution)/shard_map/ppermute | solution.py:28
  60.5 14.9 %collective-permute-start.8 = (f32[128,640]{1,0:T(8,128)S(1)}, f32[128,640]{1,0:T(8,128)S(1)}, u32[]{:S(2)}, u32[]{:S(2)}) collective-permute-start(f32[128,640]{1,0:T(8,128)S(1)} %vir_greens.2.a_ref), channel_id=1, source_target_pairs={{0,2},{2,0},{1,3},{3,1},{4,6},{6,4},{5,7},{7,5},{8,10},{10,8},{9,1... | collective-permute-start | bytes 983048 | tf_op jit(solution)/shard_map/ppermute | solution.py:28
  67.4 17.0 %collective-permute-start.18 = (f32[64,2048]{1,0:T(8,128)S(1)}, f32[64,2048]{1,0:T(8,128)S(1)}, u32[]{:S(2)}, u32[]{:S(2)}) collective-permute-start(f32[64,2048]{1,0:T(8,128)S(1)} %get-tuple-element.30), channel_id=1, source_target_pairs={{0,32},{1,5},{4,36},{5,9},{8,40},{9,13},{12,44},{13,1},{32,64},{33... | collective-permute-start | bytes 1572872 | tf_op jit(solution)/shard_map/ppermute | solution.py:38
  68.5 4.1 %collective-permute-start.9 = (f32[72,512]{1,0:T(8,128)S(1)}, f32[72,512]{1,0:T(8,128)S(1)}, u32[]{:S(2)}, u32[]{:S(2)}) collective-permute-start(f32[72,512]{1,0:T(8,128)S(1)} %picked.2.here_ref), channel_id=1, source_target_pairs={{0,2},{2,0},{1,3},{3,1},{4,6},{6,4},{5,7},{7,5},{8,10},{10,8},{9,1... | collective-permute-start | bytes 442376 | tf_op jit(solution)/shard_map/ppermute | solution.py:28
  73.5 11.7 %collective-permute-start.20 = (f32[64,2048]{1,0:T(8,128)S(1)}, f32[64,2048]{1,0:T(8,128)S(1)}, u32[]{:S(2)}, u32[]{:S(2)}) collective-permute-start(f32[64,2048]{1,0:T(8,128)S(1)} %get-tuple-element.32), channel_id=1, source_target_pairs={{0,96},{1,13},{4,100},{5,1},{8,104},{9,5},{12,108},{13,9},{32,0},{... | collective-permute-start | bytes 1572872 | tf_op jit(solution)/shard_map/ppermute | solution.py:38
  80.7 10.0 %collective-permute-start.19 = (f32[64,2048]{1,0:T(8,128)S(1)}, f32[64,2048]{1,0:T(8,128)S(1)}, u32[]{:S(2)}, u32[]{:S(2)}) collective-permute-start(f32[64,2048]{1,0:T(8,128)S(1)} %get-tuple-element.31), channel_id=1, source_target_pairs={{0,64},{1,9},{4,68},{5,13},{8,72},{9,1},{12,76},{13,5},{32,96},{33... | collective-permute-start | bytes 1572872 | tf_op jit(solution)/shard_map/ppermute | solution.py:38
  81.6 15.3 %collective-permute-start.25 = (f32[64,2048]{1,0:T(8,128)S(1)}, f32[64,2048]{1,0:T(8,128)S(1)}, u32[]{:S(2)}, u32[]{:S(2)}) collective-permute-start(f32[64,2048]{1,0:T(8,128)S(1)} %get-tuple-element.38), channel_id=1, source_target_pairs={{0,32},{1,5},{4,36},{5,9},{8,40},{9,13},{12,44},{13,1},{32,64},{33... | collective-permute-start | bytes 1572872 | tf_op jit(solution)/shard_map/ppermute | solution.py:38
  82.2 20.3 %collective-permute-start.27 = (f32[64,2048]{1,0:T(8,128)S(1)}, f32[64,2048]{1,0:T(8,128)S(1)}, u32[]{:S(2)}, u32[]{:S(2)}) collective-permute-start(f32[64,2048]{1,0:T(8,128)S(1)} %get-tuple-element.40), channel_id=1, source_target_pairs={{0,96},{1,13},{4,100},{5,1},{8,104},{9,5},{12,108},{13,9},{32,0},{... | collective-permute-start | bytes 1572872 | tf_op jit(solution)/shard_map/ppermute | solution.py:38
  84.3 18.8 %collective-permute-start.26 = (f32[64,2048]{1,0:T(8,128)S(1)}, f32[64,2048]{1,0:T(8,128)S(1)}, u32[]{:S(2)}, u32[]{:S(2)}) collective-permute-start(f32[64,2048]{1,0:T(8,128)S(1)} %get-tuple-element.39), channel_id=1, source_target_pairs={{0,64},{1,9},{4,68},{5,13},{8,72},{9,1},{12,76},{13,5},{32,96},{33... | collective-permute-start | bytes 1572872 | tf_op jit(solution)/shard_map/ppermute | solution.py:38
  91.0 21.7 %collective-permute-start.21 = (f32[16,2048]{1,0:T(8,128)S(1)}, f32[16,2048]{1,0:T(8,128)S(1)}, u32[]{:S(2)}, u32[]{:S(2)}) collective-permute-start(f32[16,2048]{1,0:T(8,128)S(1)} %get-tuple-element.33), channel_id=1, source_target_pairs={{0,0},{1,17},{4,4},{5,21},{8,8},{9,25},{12,12},{13,29},{16,16},{17... | collective-permute-start | bytes 393224 | tf_op jit(solution)/shard_map/ppermute | solution.py:64
  95.5 17.2 %collective-permute-start.22 = (f32[16,2048]{1,0:T(8,128)S(1)}, f32[16,2048]{1,0:T(8,128)S(1)}, u32[]{:S(2)}, u32[]{:S(2)}) collective-permute-start(f32[16,2048]{1,0:T(8,128)S(1)} %get-tuple-element.34), channel_id=1, source_target_pairs={{0,4},{1,49},{4,8},{5,53},{8,12},{9,57},{12,0},{13,61},{16,20},{17... | collective-permute-start | bytes 393224 | tf_op jit(solution)/shard_map/ppermute | solution.py:64
  97.0 18.1 %collective-permute-start.23 = (f32[16,2048]{1,0:T(8,128)S(1)}, f32[16,2048]{1,0:T(8,128)S(1)}, u32[]{:S(2)}, u32[]{:S(2)}) collective-permute-start(f32[16,2048]{1,0:T(8,128)S(1)} %get-tuple-element.35), channel_id=1, source_target_pairs={{0,8},{1,81},{4,12},{5,85},{8,0},{9,89},{12,4},{13,93},{16,24},{17... | collective-permute-start | bytes 393224 | tf_op jit(solution)/shard_map/ppermute | solution.py:64
  102.5 15.7 %collective-permute-start.24 = (f32[16,2048]{1,0:T(8,128)S(1)}, f32[16,2048]{1,0:T(8,128)S(1)}, u32[]{:S(2)}, u32[]{:S(2)}) collective-permute-start(f32[16,2048]{1,0:T(8,128)S(1)} %get-tuple-element.36), channel_id=1, source_target_pairs={{0,12},{1,113},{4,0},{5,117},{8,4},{9,121},{12,8},{13,125},{16,28}... | collective-permute-start | bytes 393224 | tf_op jit(solution)/shard_map/ppermute | solution.py:64
  103.5 14.7 %collective-permute-start.28 = (f32[16,2048]{1,0:T(8,128)S(1)}, f32[16,2048]{1,0:T(8,128)S(1)}, u32[]{:S(2)}, u32[]{:S(2)}) collective-permute-start(f32[16,2048]{1,0:T(8,128)S(1)} %get-tuple-element.41), channel_id=1, source_target_pairs={{0,1},{1,16},{4,5},{5,20},{8,9},{9,24},{12,13},{13,28},{16,17},{17... | collective-permute-start | bytes 393224 | tf_op jit(solution)/shard_map/ppermute | solution.py:64
  112.7 5.6 %collective-permute-start.29 = (f32[16,2048]{1,0:T(8,128)S(1)}, f32[16,2048]{1,0:T(8,128)S(1)}, u32[]{:S(2)}, u32[]{:S(2)}) collective-permute-start(f32[16,2048]{1,0:T(8,128)S(1)} %get-tuple-element.42), channel_id=1, source_target_pairs={{0,5},{1,48},{4,9},{5,52},{8,13},{9,56},{12,1},{13,60},{16,21},{17... | collective-permute-start | bytes 393224 | tf_op jit(solution)/shard_map/ppermute | solution.py:64
  112.7 7.2 %collective-permute-start.30 = (f32[16,2048]{1,0:T(8,128)S(1)}, f32[16,2048]{1,0:T(8,128)S(1)}, u32[]{:S(2)}, u32[]{:S(2)}) collective-permute-start(f32[16,2048]{1,0:T(8,128)S(1)} %get-tuple-element.43), channel_id=1, source_target_pairs={{0,9},{1,80},{4,13},{5,84},{8,1},{9,88},{12,5},{13,92},{16,25},{17... | collective-permute-start | bytes 393224 | tf_op jit(solution)/shard_map/ppermute | solution.py:64
  115.1 5.1 %collective-permute-start.31 = (f32[16,2048]{1,0:T(8,128)S(1)}, f32[16,2048]{1,0:T(8,128)S(1)}, u32[]{:S(2)}, u32[]{:S(2)}) collective-permute-start(f32[16,2048]{1,0:T(8,128)S(1)} %get-tuple-element.44), channel_id=1, source_target_pairs={{0,13},{1,112},{4,1},{5,116},{8,5},{9,120},{12,9},{13,124},{16,29}... | collective-permute-start | bytes 393224 | tf_op jit(solution)/shard_map/ppermute | solution.py:64
  (7 other events, 64.0 us)
where the time goes:
time: 123 us; the launch traced here: 121 us
  starting transfers between devices  60.7 us (49%)
  waiting for transfers between devices  28.1 us (23%)
  Pallas kernels  24.6 us (20%)
  local copies, waits for them, and re-layouts  4.28 us (3%)
  other arithmetic  2.91 us (2%)
    ppermute x8, starting transfers between devices, to_owner(): return lax.ppermute(x, PTS + ('core',), inner_pairs(by, other))  26.8 us
    ppermute x9, waiting for transfers between devices, outer_shift(): return lax.ppermute(x, ('z', 'x', 'core'), pairs)  19.6 us
    ppermute x9, starting transfers between devices, outer_shift(): return lax.ppermute(x, ('z', 'x', 'core'), pairs)  12.3 us
    pallas_call x2, Pallas kernels, vir_greens(): pl.pallas_call(body, grid=(2 * per,), in_specs=[whole(b) for b in blocks]...  11.4 us
    ppermute x10, starting transfers between devices, swap(): return lax.ppermute(x, axis, [(0, 1), (1, 0)])  10.8 us
    pallas_call x2, Pallas kernels, projections(): pl.pallas_call(body, grid=(2 * per,), in_specs=[whole] * 3 + [pl.BlockSpe...  10.6 us
    ppermute x3, starting transfers between devices, inner_shift(): return lax.ppermute(x, ('z', 'x', 'core'), pairs)  5.85 us
    ppermute x2, starting transfers between devices, from_owner(): return lax.ppermute(x, PTS + ('core',), pairs)  4.94 us
  transfers between devices with their start and end apart: 32, of which 9 were waited for; matrix products, arithmetic and copies ran while one was open for 2% of the time, Pallas kernels for 20%

commit v1 on v0

--- a/solution.py
+++ b/solution.py
@@ -130,9 +130,27 @@
     )
 
 
-def contract_parts(stacked, right):
+def split(x):
+    rows, width = x.shape
+    step = 768 if width % 768 == 0 else width
+
+    def body(ref, high, low):
+        high[...], low[...] = parts(ref[...])
+
+    spec = pl.BlockSpec((rows, step), lambda i: (0, i))
+    return pl.pallas_call(
+        body,
+        grid=(width // step,),
+        in_specs=[spec],
+        out_specs=[spec] * 2,
+        out_shape=[jax.ShapeDtypeStruct(x.shape, jnp.bfloat16)] * 2,
+        compiler_params=limit(12),
+        name="split",
+    )(x)
+
+
+def contract_parts(stacked, high, low):
     rows = stacked.shape[0] // 2
-    high, low = parts(right)
     both = contract(stacked, high)
     return (both[:rows] + both[rows:]) + contract(stacked[:rows], low)
 
@@ -149,8 +167,8 @@
 
     def body(*refs):
         ins, w_ref = refs[:n], refs[n]
-        sets = refs[n + 1 : n + 3]
-        out, stacked = refs[n + 3 :]
+        sets = refs[n + 1 : n + 5]
+        out, stacked = refs[n + 5 :]
         i = pl.program_id(0)
 
         @pl.when(i == 0)
@@ -170,7 +188,7 @@
                         high, low = parts(x * w[t : t + 1])
                         stacked[pl.ds(at, rows), :] = high
                         stacked[pl.ds(total + at, rows), :] = low
-                out[...] += contract_parts(stacked[...], sets[s][...])
+                out[...] += contract_parts(stacked[...], sets[2 * s][...], sets[2 * s + 1][...])
 
     whole = lambda a: pl.BlockSpec(a.shape, lambda i: (0, 0))
     return pl.pallas_call(
@@ -180,6 +198,8 @@
         + [whole(weight)]
         + [
             pl.BlockSpec((points, step), lambda i: (0, jnp.minimum(i, per - 1))),
+            pl.BlockSpec((points, step), lambda i: (0, jnp.minimum(i, per - 1))),
+            pl.BlockSpec((points, step), lambda i: (0, jnp.maximum(i - per, 0))),
             pl.BlockSpec((points, step), lambda i: (0, jnp.maximum(i - per, 0))),
         ],
         out_specs=pl.BlockSpec((total, points), lambda i: (0, 0)),
@@ -210,7 +230,7 @@
                 stacked[pl.ds(t * columns, columns), k] = high
                 stacked[pl.ds((2 + t) * columns, columns), k] = low
         for i in range(4):
-            part = contract_parts(stacked[:, pl.ds(i * count, count)], sets[i][...])
+            part = contract_parts(stacked[:, pl.ds(i * count, count)], *parts(sets[i][...]))
             total = part if total is None else total + part
         out[...] = total
 
@@ -223,20 +243,18 @@
     )(here, there, *point_sets)
 
 
-def projections(vir_here, vir_there, occ, wave_sets, own):
+def projections(vir_here, vir_there, occ, waves, own):
     rows, points = occ.shape
-    waves = wave_sets[0].shape[0]
+    count = waves.shape[0]
     step = 512
-    per = waves // step
     blocks = rows // (2 * own * SIDE)
     share = rows // blocks
     inner = share // (2 * own)
 
-    def body(a_ref, b_ref, o_ref, w_first, w_last, *refs):
+    def body(a_ref, b_ref, o_ref, w_ref, *refs):
         outs, stacked = refs[:-1], refs[-1]
-        i = pl.program_id(0)
-
-        @pl.when(i == 0)
+
+        @pl.when(pl.program_id(0) == 0)
         def _():
             response = -(o_ref[...] * (a_ref[...] + b_ref[...]))
             early, late = response[: rows // 2], response[rows // 2 :]
@@ -247,35 +265,24 @@
                 stacked[pl.ds(2 * own * j, 2 * own), :] = high
                 stacked[pl.ds(rows + 2 * own * j, 2 * own), :] = low
 
-        for s, w_ref in enumerate((w_first, w_last)):
-
-            @pl.when(i // per == s)
-            def _(s=s, w_ref=w_ref):
-                result = contract_parts(stacked[...], w_ref[...])
-                for d in range(blocks):
-                    outs[s * blocks + d][...] = result[d * share : (d + 1) * share]
+        result = contract_parts(stacked[...], *parts(w_ref[...]))
+        for d in range(blocks):
+            outs[d][...] = result[d * share : (d + 1) * share]
 
     whole = pl.BlockSpec((rows, points), lambda i: (0, 0))
-    first = lambda i: jnp.minimum(i, per - 1)
-    last = lambda i: jnp.maximum(i - per, 0)
-    return pl.pallas_call(
-        body,
-        grid=(2 * per,),
-        in_specs=[whole] * 3
-        + [
-            pl.BlockSpec((step, points), lambda i: (first(i), 0)),
-            pl.BlockSpec((step, points), lambda i: (last(i), 0)),
-        ],
-        out_specs=[pl.BlockSpec((share, step), lambda i: (0, first(i)))] * blocks
-        + [pl.BlockSpec((share, step), lambda i: (0, last(i)))] * blocks,
-        out_shape=[jax.ShapeDtypeStruct((share, waves), jnp.float32)] * (2 * blocks),
+    return pl.pallas_call(
+        body,
+        grid=(count // step,),
+        in_specs=[whole] * 3 + [pl.BlockSpec((step, points), lambda i: (i, 0))],
+        out_specs=[pl.BlockSpec((share, step), lambda i: (0, i))] * blocks,
+        out_shape=[jax.ShapeDtypeStruct((share, count), jnp.float32)] * blocks,
         scratch_shapes=[pltpu.VMEM((2 * rows, points), jnp.bfloat16)],
         compiler_params=limit(24),
         cost_estimate=pl.CostEstimate(
-            flops=12 * rows * points * waves, bytes_accessed=14_000_000, transcendentals=0
+            flops=6 * rows * points * count, bytes_accessed=8_000_000, transcendentals=0
         ),
         name="projections",
-    )(vir_here, vir_there, occ, *wave_sets)
+    )(vir_here, vir_there, occ, waves)
 
 
 def summed_blocks(arrays):
@@ -314,11 +321,13 @@
     moments = jnp.array(IMAG_TIMES, jnp.float32)
 
     cols = joined([occ_cols, vir_cols], 1)
-    block = joined([from_owner(cols, 0, other) for other in (False, True)], 1)
-    occ_points_there = swap(after(occ_points, block), "yl")
+    block = [from_owner(cols, 0, other) for other in (False, True)]
+    block = joined(block, 1)
     block = joined([block] + [inner_shift(block, -d) for d in range(1, SIDE)], 0)
     blocks = [block] + [None] * (SIDE - 1)
     for d in (1, 3, 2):
+        if d == 2:
+            block = after(block, (blocks[1], blocks[3]))
         blocks[d] = outer_shift(block, -d)
 
     energy = jnp.concatenate([occ_energy, vir_energy])
@@ -327,30 +336,35 @@
     vir_weight = jnp.exp(-moments[:, None] * vir_both[None, :])
     occ_chip = jnp.concatenate([occ_energy, energy_other[:occ_count]])
     occ_chip = jnp.broadcast_to(occ_chip[None], (8, 2 * occ_count))
-    vir_sets = (vir_points, swap(vir_points, "core"))
-    occ_sets = None
+    occ_points_there = swap(occ_points, "yl")
+    vir_sets = list(split(vir_points))
+    vir_other = swap(vir_points, "core")
+    vir_sets += list(split(vir_other))
+    occ_near = after(occ_points, (blocks[1], blocks[3]))
+    occ_sets = [occ_near, swap(occ_near, "core")]
 
     sums = [[None] * SIDE for _ in range(2)]
-    for group in ((1, 3), (0, 2)):
+    for n, group in enumerate(((1, 3), (0, 2))):
         pair = [blocks[d] for d in group]
         occ_here = picked(pair, occ_chip, occ_count, cols.shape[1])
         occ_there = swap(occ_here, "yl")
         vir_here = vir_greens(pair, vir_weight, vir_sets, occ_count)
         vir_there = swap(vir_here, "yl")
-        if occ_sets is None:
-            near, far, waves = after((occ_points, occ_points_there, plane_waves), vir_here)
-            occ_sets = (near, swap(near, "core"), far, swap(far, "core"))
+        if n == 0:
+            occ_far, waves = after((occ_points_there, plane_waves), vir_here)
+            occ_sets += [occ_far, swap(occ_far, "core")]
             wave_sets = (plane_waves, swap(waves, "core"))
         occ_green = occ_greens(occ_here, occ_there, occ_sets)
-        found = projections(vir_here, vir_there, occ_green, wave_sets, own)
         for s in range(2):
+            found = projections(vir_here, vir_there, occ_green, wave_sets[s], own)
             for j, d in enumerate(group):
-                sums[s][d] = outer_shift(found[2 * s + j], d) if d else found[2 * s + j]
+                sums[s][d] = outer_shift(found[j], d) if d else found[j]
 
     results = []
     for s, other in enumerate((False, True)):
         finished = summed_blocks(sums[s])
-        results += [to_owner(finished[d], d, other) for d in range(SIDE)]
+        for d in range(SIDE):
+            results.append(to_owner(finished[d], d, other))
     total = sum(results[1:], results[0])
     return jnp.transpose(total.reshape(2, own, -1), (0, 2, 1))
 

time: 123 us -> 118 us (0.959)
  starting transfers between devices: 60.7 us -> 52.6 us
  Pallas kernels: 24.6 us -> 27.6 us
  waiting for transfers between devices: 28.1 us -> 30.5 us
  other arithmetic: 2.91 us -> 1.53 us
    ppermute x8, starting transfers between devices: 26.8 us -> 22.6 us  [to_owner(): return lax.ppermute(x, PTS + ('core',), inner_pairs(by, other))]
    ppermute x10, starting transfers between devices: 10.8 us -> 6.63 us  [swap(): return lax.ppermute(x, axis, [(0, 1), (1, 0)])]
    pallas_call x2 -> x6, Pallas kernels: 10.6 us -> 13.7 us  [the longest x4 10.3 us: projections(): pl.pallas_call(body, grid=(count // step,), in_specs=[whole] * 3 + [pl.Bl...]
    ppermute x2, waiting for transfers between devices: 3.01 us -> 5.36 us  [from_owner(): return lax.ppermute(x, PTS + ('core',), pairs)]
    ppermute x9, starting transfers between devices: 12.3 us -> 13.7 us  [outer_shift(): return lax.ppermute(x, ('z', 'x', 'core'), pairs)]
    ppermute x3, starting transfers between devices: 5.85 us -> 4.53 us  [inner_shift(): return lax.ppermute(x, ('z', 'x', 'core'), pairs)]
    unnamed x14 -> x18, local copies, waits for them, and re-layouts: 4.27 us -> 4.27 us
  transfers between devices with their start and end apart: 32 -> 32, of which waited for: 9 -> 10; matrix products, arithmetic and copies ran while one was open for 2% -> 1% of each run, Pallas kernels for 20% -> 24%
where the time goes in v1:
time: 118 us; the launch traced here: 117 us
  starting transfers between devices  52.6 us (45%)
  waiting for transfers between devices  30.5 us (26%)
  Pallas kernels  27.6 us (23%)
  local copies, waits for them, and re-layouts  4.28 us (4%)
  other arithmetic  1.53 us (1%)
    ppermute x8, starting transfers between devices, to_owner(): return lax.ppermute(x, PTS + ('core',), inner_pairs(by, other))  22.6 us
    ppermute x9, waiting for transfers between devices, outer_shift(): return lax.ppermute(x, ('z', 'x', 'core'), pairs)  18.9 us
    ppermute x9, starting transfers between devices, outer_shift(): return lax.ppermute(x, ('z', 'x', 'core'), pairs)  13.7 us
    pallas_call x2, Pallas kernels, vir_greens(): pl.pallas_call(body, grid=(2 * per,), in_specs=[whole(b) for b in blocks]...  11.3 us
    pallas_call x4, Pallas kernels, projections(): pl.pallas_call(body, grid=(count // step,), in_specs=[whole] * 3 + [pl.Bl...  10.3 us
    ppermute x10, starting transfers between devices, swap(): return lax.ppermute(x, axis, [(0, 1), (1, 0)])  6.63 us
    ppermute x2, waiting for transfers between devices, from_owner(): return lax.ppermute(x, PTS + ('core',), pairs)  5.36 us
    ppermute x2, starting transfers between devices, from_owner(): return lax.ppermute(x, PTS + ('core',), pairs)  5.14 us
  transfers between devices with their start and end apart: 32, of which 10 were waited for; matrix products, arithmetic and copies ran while one was open for 1% of the time, Pallas kernels for 24%

profile of v1, /device:TPU:1, one launch (start us, length us, event | category | flops | bytes accessed | tf_op | source)
XLA Modules:
  0.0 116.9 jit_solution(7272563419747129016)
XLA Ops:
  0.0 1.4 %collective-permute-start.9 = (f32[640,2304]{1,0:T(8,128)}, f32[640,2304]{1,0:T(8,128)S(1)}, u32[]{:S(2)}, u32[]{:S(2)}) collective-permute-start(f32[640,2304]{1,0:T(8,128)} %ref.1), channel_id=1, source_target_pairs={{0,1},{1,0},{2,3},{3,2},{4,5},{5,4},{6,7},{7,6},{8,9},{9,8},{10,11... | collective-permute-start | bytes 17694728 | tf_op jit(solution)/shard_map/ppermute | solution.py:28
  3.0 5.1 %collective-permute-start = (f32[8,2560]{1,0:T(8,128)S(1)}, f32[8,2560]{1,0:T(8,128)S(1)}, u32[]{:S(2)}, u32[]{:S(2)}) collective-permute-start(f32[8,2560]{1,0:T(8,128)S(1)} %joined.3), channel_id=1, source_target_pairs={{0,0},{17,1},{4,4},{21,5},{8,8},{25,9},{12,12},{29,13},{16,16},{1,... | collective-permute-start | bytes 245768 | tf_op jit(solution)/shard_map/ppermute | solution.py:69
  8.1 1.7 %collective-permute-done.refs_0_ = f32[8,2560]{1,0:T(8,128)S(1)} collective-permute-done((f32[8,2560]{1,0:T(8,128)S(1)}, f32[8,2560]{1,0:T(8,128)S(1)}, u32[]{:S(2)}, u32[]{:S(2)}) %collective-permute-start) | collective-permute-done | bytes 81952 | tf_op jit(solution)/shard_map/ppermute | solution.py:69
  9.9 3.6 %collective-permute-done.1.refs_1_ = f32[8,2560]{1,0:T(8,128)S(1)} collective-permute-done((f32[8,2560]{1,0:T(8,128)S(1)}, f32[8,2560]{1,0:T(8,128)S(1)}, u32[]{:S(2)}, u32[]{:S(2)}) %collective-permute-start.1) | collective-permute-done | bytes 81952 | tf_op jit(solution)/shard_map/ppermute | solution.py:69
  13.5 3.8 %collective-permute-start.2 = (f32[8,5120]{1,0:T(8,128)S(1)}, f32[8,5120]{1,0:T(8,128)S(1)}, u32[]{:S(2)}, u32[]{:S(2)}) collective-permute-start(f32[8,5120]{1,0:T(8,128)S(1)} %joined.4.refs_0_), channel_id=1, source_target_pairs={{0,12},{1,97},{4,0},{5,101},{8,4},{9,105},{12,8},{13,109},{32,44},... | collective-permute-start | bytes 491528 | tf_op jit(solution)/shard_map/ppermute | solution.py:48
  18.8 2.7 %copy-done = f32[640,2304]{1,0:T(8,128)S(1)} copy-done((f32[640,2304]{1,0:T(8,128)S(1)}, f32[640,2304]{1,0:T(8,128)}, u32[]{:S(2)}) %copy-start) | copy-done | bytes 5898264
  21.4 1.6 %split.2 = (bf16[640,2304]{1,0:T(8,128)(2,1)S(1)}, bf16[640,2304]{1,0:T(8,128)(2,1)S(1)}) custom-call(f32[640,2304]{1,0:T(8,128)S(1)} %copy-done), custom_call_target="tpu_custom_call" | custom-call | tf_op jit(solution)/shard_map/split/pallas_call | solution.py:141
  24.5 2.5 %collective-permute-start.5 = (f32[32,5120]{1,0:T(8,128)S(1)}, f32[32,5120]{1,0:T(8,128)S(1)}, u32[]{:S(2)}, u32[]{:S(2)}) collective-permute-start(f32[32,5120]{1,0:T(8,128)S(1)} %joined.5.refs_0_.refs_1_), channel_id=1, source_target_pairs={{0,96},{1,13},{4,100},{5,1},{8,104},{9,5},{12,108},{13,9},{32,0},{... | collective-permute-start | bytes 1966088 | tf_op jit(solution)/shard_map/ppermute | solution.py:38
  27.2 1.7 %split.3 = (bf16[640,2304]{1,0:T(8,128)(2,1)S(1)}, bf16[640,2304]{1,0:T(8,128)(2,1)S(1)}) custom-call(f32[640,2304]{1,0:T(8,128)S(1)} %collective-permute-done.9.ref), custom_call_target="tpu_custom_call" | custom-call | tf_op jit(solution)/shard_map/split/pallas_call | solution.py:141
  28.9 5.7 %collective-permute-done.5.refs_0_.refs_1_ = f32[32,5120]{1,0:T(8,128)S(1)} collective-permute-done((f32[32,5120]{1,0:T(8,128)S(1)}, f32[32,5120]{1,0:T(8,128)S(1)}, u32[]{:S(2)}, u32[]{:S(2)}) %collective-permute-start.5) | collective-permute-done | bytes 655392 | tf_op jit(solution)/shard_map/ppermute | solution.py:38
  34.6 3.4 %collective-permute-done.6.refs_1_.refs_2_.refs_3_ = f32[32,5120]{1,0:T(8,128)S(1)} collective-permute-done((f32[32,5120]{1,0:T(8,128)S(1)}, f32[32,5120]{1,0:T(8,128)S(1)}, u32[]{:S(2)}, u32[]{:S(2)}) %collective-permute-start.6) | collective-permute-done | bytes 655392 | tf_op jit(solution)/shard_map/ppermute | solution.py:38
  38.0 5.7 %vir_greens.3.a_ref = f32[128,640]{1,0:T(8,128)S(1)} custom-call(f32[32,5120]{1,0:T(8,128)S(1)} %collective-permute-done.5.refs_0_.refs_1_, f32[32,5120]{1,0:T(8,128)S(1)} %collective-permute-done.6.refs_1_.refs_2_.refs_3_, f32[2,4608]{1,0:T(2,128)S(1)} %multiply_exponential_fusion.refs_2_, bf16[640,2304]{1,0:T(8,128)(2,1)S(1)} %get-tuple-element.30.refs_3_, ...), custom_call_target="tpu_custom_call" | custom-call | flops 2264924160 | bytes 14000000 | tf_op jit(solution)/shard_map/vir_greens/pallas_call | solution.py:194
  44.6 2.5 %collective-permute-start.7 = (f32[32,5120]{1,0:T(8,128)S(1)}, f32[32,5120]{1,0:T(8,128)S(1)}, u32[]{:S(2)}, u32[]{:S(2)}) collective-permute-start(f32[32,5120]{1,0:T(8,128)S(1)} %joined.5.refs_0_.refs_1_), channel_id=1, source_target_pairs={{0,64},{1,9},{4,68},{5,13},{8,72},{9,1},{12,76},{13,5},{32,96},{33... | collective-permute-start | bytes 1966088 | tf_op jit(solution)/shard_map/ppermute | solution.py:38
  48.8 7.1 %collective-permute-done.7.refs_1_.refs_2_.refs_3_ = f32[32,5120]{1,0:T(8,128)S(1)} collective-permute-done((f32[32,5120]{1,0:T(8,128)S(1)}, f32[32,5120]{1,0:T(8,128)S(1)}, u32[]{:S(2)}, u32[]{:S(2)}) %collective-permute-start.7) | collective-permute-done | bytes 655392 | tf_op jit(solution)/shard_map/ppermute | solution.py:38
  55.8 1.3 %collective-permute-start.16 = (f32[72,512]{1,0:T(8,128)S(1)}, f32[72,512]{1,0:T(8,128)S(1)}, u32[]{:S(2)}, u32[]{:S(2)}) collective-permute-start(f32[72,512]{1,0:T(8,128)S(1)} %picked.3.here_ref), channel_id=1, source_target_pairs={{0,2},{2,0},{1,3},{3,1},{4,6},{6,4},{5,7},{7,5},{8,10},{10,8},{9,1... | collective-permute-start | bytes 442376 | tf_op jit(solution)/shard_map/ppermute | solution.py:28
  57.1 5.7 %vir_greens.2.a_ref = f32[128,640]{1,0:T(8,128)S(1)} custom-call(f32[32,5120]{1,0:T(8,128)S(1)} %joined.5.refs_0_.refs_1_, f32[32,5120]{1,0:T(8,128)S(1)} %collective-permute-done.7.refs_1_.refs_2_.refs_3_, f32[2,4608]{1,0:T(2,128)S(1)} %multiply_exponential_fusion.refs_2_, bf16[640,2304]{1,0:T(8,128)(2,1)S(1)} %get-tuple-element.30.refs_3_, ...), custom_call_target="tpu_custom_call" | custom-call | flops 2264924160 | bytes 14000000 | tf_op jit(solution)/shard_map/vir_greens/pallas_call | solution.py:194
  64.0 2.6 %projections.5 = (f32[64,2048]{1,0:T(8,128)S(1)}, f32[64,2048]{1,0:T(8,128)S(1)}) custom-call(f32[128,640]{1,0:T(8,128)S(1)} %vir_greens.3.a_ref, f32[128,640]{1,0:T(8,128)S(1)} %collective-permute-done.15.b_ref, f32[128,640]{1,0:T(8,128)S(1)} %occ_greens.3.o_ref, f32[2048,640]{1,0:T(8,128)S(1)} %bitcast.5), custom_call_target="tpu_custom_call" | custom-call | flops 1006632960 | bytes 8000000 | tf_op jit(solution)/shard_map/projections/pallas_call | solution.py:273
  66.6 1.5 %collective-permute-start.17 = (f32[64,2048]{1,0:T(8,128)S(1)}, f32[64,2048]{1,0:T(8,128)S(1)}, u32[]{:S(2)}, u32[]{:S(2)}) collective-permute-start(f32[64,2048]{1,0:T(8,128)S(1)} %get-tuple-element.37), channel_id=1, source_target_pairs={{0,32},{1,5},{4,36},{5,9},{8,40},{9,13},{12,44},{13,1},{32,64},{33... | collective-permute-start | bytes 1572872 | tf_op jit(solution)/shard_map/ppermute | solution.py:38
  68.9 1.9 %collective-permute-start.19 = (f32[64,2048]{1,0:T(8,128)S(1)}, f32[64,2048]{1,0:T(8,128)S(1)}, u32[]{:S(2)}, u32[]{:S(2)}) collective-permute-start(f32[64,2048]{1,0:T(8,128)S(1)} %get-tuple-element.39), channel_id=1, source_target_pairs={{0,96},{1,13},{4,100},{5,1},{8,104},{9,5},{12,108},{13,9},{32,0},{... | collective-permute-start | bytes 1572872 | tf_op jit(solution)/shard_map/ppermute | solution.py:38
  70.8 3.3 %collective-permute-done.11.there_ref = f32[72,512]{1,0:T(8,128)S(1)} collective-permute-done((f32[72,512]{1,0:T(8,128)S(1)}, f32[72,512]{1,0:T(8,128)S(1)}, u32[]{:S(2)}, u32[]{:S(2)}) %collective-permute-start.11) | collective-permute-done | bytes 147488 | tf_op jit(solution)/shard_map/ppermute | solution.py:28
  75.0 2.6 %projections.4 = (f32[64,2048]{1,0:T(8,128)S(1)}, f32[64,2048]{1,0:T(8,128)S(1)}) custom-call(f32[128,640]{1,0:T(8,128)S(1)} %vir_greens.2.a_ref, f32[128,640]{1,0:T(8,128)S(1)} %collective-permute-done.10.b_ref, f32[128,640]{1,0:T(8,128)S(1)} %occ_greens.2.o_ref, f32[2048,640]{1,0:T(8,128)S(1)} %bitcast.5), custom_call_target="tpu_custom_call" | custom-call | flops 1006632960 | bytes 8000000 | tf_op jit(solution)/shard_map/projections/pallas_call | solution.py:273
  77.6 2.4 %collective-permute-start.18 = (f32[64,2048]{1,0:T(8,128)S(1)}, f32[64,2048]{1,0:T(8,128)S(1)}, u32[]{:S(2)}, u32[]{:S(2)}) collective-permute-start(f32[64,2048]{1,0:T(8,128)S(1)} %get-tuple-element.38), channel_id=1, source_target_pairs={{0,64},{1,9},{4,68},{5,13},{8,72},{9,1},{12,76},{13,5},{32,96},{33... | collective-permute-start | bytes 1572872 | tf_op jit(solution)/shard_map/ppermute | solution.py:38
  80.0 2.6 %projections.7 = (f32[64,2048]{1,0:T(8,128)S(1)}, f32[64,2048]{1,0:T(8,128)S(1)}) custom-call(f32[128,640]{1,0:T(8,128)S(1)} %vir_greens.3.a_ref, f32[128,640]{1,0:T(8,128)S(1)} %collective-permute-done.15.b_ref, f32[128,640]{1,0:T(8,128)S(1)} %occ_greens.3.o_ref, f32[2048,640]{1,0:T(8,128)S(1)} %collective-permute-done.24.w_ref), custom_call_target="tpu_custom_call" | custom-call | flops 1006632960 | bytes 8000000 | tf_op jit(solution)/shard_map/projections/pallas_call | solution.py:273
  83.0 2.4 %collective-permute-start.27 = (f32[64,2048]{1,0:T(8,128)S(1)}, f32[64,2048]{1,0:T(8,128)S(1)}, u32[]{:S(2)}, u32[]{:S(2)}) collective-permute-start(f32[64,2048]{1,0:T(8,128)S(1)} %get-tuple-element.48), channel_id=1, source_target_pairs={{0,96},{1,13},{4,100},{5,1},{8,104},{9,5},{12,108},{13,9},{32,0},{... | collective-permute-start | bytes 1572872 | tf_op jit(solution)/shard_map/ppermute | solution.py:38
  85.4 2.6 %projections.6 = (f32[64,2048]{1,0:T(8,128)S(1)}, f32[64,2048]{1,0:T(8,128)S(1)}) custom-call(f32[128,640]{1,0:T(8,128)S(1)} %vir_greens.2.a_ref, f32[128,640]{1,0:T(8,128)S(1)} %collective-permute-done.10.b_ref, f32[128,640]{1,0:T(8,128)S(1)} %occ_greens.2.o_ref, f32[2048,640]{1,0:T(8,128)S(1)} %collective-permute-done.24.w_ref), custom_call_target="tpu_custom_call" | custom-call | flops 1006632960 | bytes 8000000 | tf_op jit(solution)/shard_map/projections/pallas_call | solution.py:273
  88.4 4.0 %collective-permute-start.20 = (f32[16,2048]{1,0:T(8,128)S(1)}, f32[16,2048]{1,0:T(8,128)S(1)}, u32[]{:S(2)}, u32[]{:S(2)}) collective-permute-start(f32[16,2048]{1,0:T(8,128)S(1)} %get-tuple-element.40), channel_id=1, source_target_pairs={{0,0},{1,17},{4,4},{5,21},{8,8},{9,25},{12,12},{13,29},{16,16},{17... | collective-permute-start | bytes 393224 | tf_op jit(solution)/shard_map/ppermute | solution.py:64
  93.2 2.7 %collective-permute-start.22 = (f32[16,2048]{1,0:T(8,128)S(1)}, f32[16,2048]{1,0:T(8,128)S(1)}, u32[]{:S(2)}, u32[]{:S(2)}) collective-permute-start(f32[16,2048]{1,0:T(8,128)S(1)} %get-tuple-element.42), channel_id=1, source_target_pairs={{0,8},{1,81},{4,12},{5,85},{8,0},{9,89},{12,4},{13,93},{16,24},{17... | collective-permute-start | bytes 393224 | tf_op jit(solution)/shard_map/ppermute | solution.py:64
  95.9 2.3 %collective-permute-start.23 = (f32[16,2048]{1,0:T(8,128)S(1)}, f32[16,2048]{1,0:T(8,128)S(1)}, u32[]{:S(2)}, u32[]{:S(2)}) collective-permute-start(f32[16,2048]{1,0:T(8,128)S(1)} %get-tuple-element.43), channel_id=1, source_target_pairs={{0,12},{1,113},{4,0},{5,117},{8,4},{9,121},{12,8},{13,125},{16,28}... | collective-permute-start | bytes 393224 | tf_op jit(solution)/shard_map/ppermute | solution.py:64
  98.2 2.0 %collective-permute-done.26.refs_2_ = f32[64,2048]{1,0:T(8,128)S(1)} collective-permute-done((f32[64,2048]{1,0:T(8,128)S(1)}, f32[64,2048]{1,0:T(8,128)S(1)}, u32[]{:S(2)}, u32[]{:S(2)}) %collective-permute-start.26) | collective-permute-done | bytes 524320 | tf_op jit(solution)/shard_map/ppermute | solution.py:38
  100.5 8.3 %collective-permute-start.28 = (f32[16,2048]{1,0:T(8,128)S(1)}, f32[16,2048]{1,0:T(8,128)S(1)}, u32[]{:S(2)}, u32[]{:S(2)}) collective-permute-start(f32[16,2048]{1,0:T(8,128)S(1)} %get-tuple-element.49), channel_id=1, source_target_pairs={{0,1},{1,16},{4,5},{5,20},{8,9},{9,24},{12,13},{13,28},{16,17},{17... | collective-permute-start | bytes 393224 | tf_op jit(solution)/shard_map/ppermute | solution.py:64
  109.5 4.6 %collective-permute-start.31 = (f32[16,2048]{1,0:T(8,128)S(1)}, f32[16,2048]{1,0:T(8,128)S(1)}, u32[]{:S(2)}, u32[]{:S(2)}) collective-permute-start(f32[16,2048]{1,0:T(8,128)S(1)} %get-tuple-element.52), channel_id=1, source_target_pairs={{0,13},{1,112},{4,1},{5,116},{8,5},{9,120},{12,9},{13,124},{16,29}... | collective-permute-start | bytes 393224 | tf_op jit(solution)/shard_map/ppermute | solution.py:64
  114.1 2.1 %collective-permute-done.29 = f32[16,2048]{1,0:T(8,128)S(1)} collective-permute-done((f32[16,2048]{1,0:T(8,128)S(1)}, f32[16,2048]{1,0:T(8,128)S(1)}, u32[]{:S(2)}, u32[]{:S(2)}) %collective-permute-start.29) | collective-permute-done | bytes 131104 | tf_op jit(solution)/shard_map/ppermute | solution.py:64
  (76 shorter events, 13.2 us)
Async XLA Ops:
  0.0 27.2 %collective-permute-start.9 = (f32[640,2304]{1,0:T(8,128)}, f32[640,2304]{1,0:T(8,128)S(1)}, u32[]{:S(2)}, u32[]{:S(2)}) collective-permute-start(f32[640,2304]{1,0:T(8,128)} %ref.1), channel_id=1, source_target_pairs={{0,1},{1,0},{2,3},{3,2},{4,5},{5,4},{6,7},{7,6},{8,9},{9,8},{10,11... | collective-permute-start | bytes 17694728 | tf_op jit(solution)/shard_map/ppermute | solution.py:28
  3.0 6.9 %collective-permute-start = (f32[8,2560]{1,0:T(8,128)S(1)}, f32[8,2560]{1,0:T(8,128)S(1)}, u32[]{:S(2)}, u32[]{:S(2)}) collective-permute-start(f32[8,2560]{1,0:T(8,128)S(1)} %joined.3), channel_id=1, source_target_pairs={{0,0},{17,1},{4,4},{21,5},{8,8},{25,9},{12,12},{29,13},{16,16},{1,... | collective-permute-start | bytes 245768 | tf_op jit(solution)/shard_map/ppermute | solution.py:69
  8.1 5.4 %collective-permute-start.1 = (f32[8,2560]{1,0:T(8,128)S(1)}, f32[8,2560]{1,0:T(8,128)S(1)}, u32[]{:S(2)}, u32[]{:S(2)}) collective-permute-start(f32[8,2560]{1,0:T(8,128)S(1)} %joined.3), channel_id=1, source_target_pairs={{1,0},{16,1},{5,4},{20,5},{9,8},{24,9},{13,12},{28,13},{17,16},{0,... | collective-permute-start | bytes 245768 | tf_op jit(solution)/shard_map/ppermute | solution.py:69
  13.5 10.1 %collective-permute-start.2 = (f32[8,5120]{1,0:T(8,128)S(1)}, f32[8,5120]{1,0:T(8,128)S(1)}, u32[]{:S(2)}, u32[]{:S(2)}) collective-permute-start(f32[8,5120]{1,0:T(8,128)S(1)} %joined.4.refs_0_), channel_id=1, source_target_pairs={{0,12},{1,97},{4,0},{5,101},{8,4},{9,105},{12,8},{13,109},{32,44},... | collective-permute-start | bytes 491528 | tf_op jit(solution)/shard_map/ppermute | solution.py:48
  17.3 6.3 %collective-permute-start.3 = (f32[8,5120]{1,0:T(8,128)S(1)}, f32[8,5120]{1,0:T(8,128)S(1)}, u32[]{:S(2)}, u32[]{:S(2)}) collective-permute-start(f32[8,5120]{1,0:T(8,128)S(1)} %joined.4.refs_0_), channel_id=1, source_target_pairs={{0,8},{1,65},{4,12},{5,69},{8,0},{9,73},{12,4},{13,77},{32,40},{33... | collective-permute-start | bytes 491528 | tf_op jit(solution)/shard_map/ppermute | solution.py:48
  17.3 7.1 %collective-permute-start.4 = (f32[8,5120]{1,0:T(8,128)S(1)}, f32[8,5120]{1,0:T(8,128)S(1)}, u32[]{:S(2)}, u32[]{:S(2)}) collective-permute-start(f32[8,5120]{1,0:T(8,128)S(1)} %joined.4.refs_0_), channel_id=1, source_target_pairs={{0,4},{1,33},{4,8},{5,37},{8,12},{9,41},{12,0},{13,45},{32,36},{33... | collective-permute-start | bytes 491528 | tf_op jit(solution)/shard_map/ppermute | solution.py:48
  18.8 4.3 %collective-permute-start.8 = (f32[2560]{0:T(1024)S(1)}, f32[2560]{0:T(1024)S(1)}, u32[]{:S(2)}, u32[]{:S(2)}) collective-permute-start(f32[2560]{0:T(1024)S(1)} %pad_maximum_fusion.1), channel_id=1, source_target_pairs={{0,1},{1,0},{2,3},{3,2},{4,5},{5,4},{6,7},{7,6},{8,9},{9,8},{10,11... | collective-permute-start | bytes 30728 | tf_op jit(solution)/shard_map/ppermute | solution.py:28
  23.1 20.6 %collective-permute-start.13 = (f32[640,256]{1,0:T(8,128)S(1)}, f32[640,256]{1,0:T(8,128)S(1)}, u32[]{:S(2)}, u32[]{:S(2)}) collective-permute-start(f32[640,256]{1,0:T(8,128)S(1)} %copy-done.1), channel_id=1, source_target_pairs={{0,2},{2,0},{1,3},{3,1},{4,6},{6,4},{5,7},{7,5},{8,10},{10,8},{9,1... | collective-permute-start | bytes 1966088 | tf_op jit(solution)/shard_map/ppermute | solution.py:28
  24.5 10.1 %collective-permute-start.5 = (f32[32,5120]{1,0:T(8,128)S(1)}, f32[32,5120]{1,0:T(8,128)S(1)}, u32[]{:S(2)}, u32[]{:S(2)}) collective-permute-start(f32[32,5120]{1,0:T(8,128)S(1)} %joined.5.refs_0_.refs_1_), channel_id=1, source_target_pairs={{0,96},{1,13},{4,100},{5,1},{8,104},{9,5},{12,108},{13,9},{32,0},{... | collective-permute-start | bytes 1966088 | tf_op jit(solution)/shard_map/ppermute | solution.py:38
  27.1 10.9 %collective-permute-start.6 = (f32[32,5120]{1,0:T(8,128)S(1)}, f32[32,5120]{1,0:T(8,128)S(1)}, u32[]{:S(2)}, u32[]{:S(2)}) collective-permute-start(f32[32,5120]{1,0:T(8,128)S(1)} %joined.5.refs_0_.refs_1_), channel_id=1, source_target_pairs={{0,32},{1,5},{4,36},{5,9},{8,40},{9,13},{12,44},{13,1},{32,64},{33... | collective-permute-start | bytes 1966088 | tf_op jit(solution)/shard_map/ppermute | solution.py:38
  43.7 36.3 %collective-permute-start.24 = (f32[2048,640]{1,0:T(8,128)S(1)}, f32[2048,640]{1,0:T(8,128)S(1)}, u32[]{:S(2)}, u32[]{:S(2)}) collective-permute-start(f32[2048,640]{1,0:T(8,128)S(1)} %bitcast.5), channel_id=1, source_target_pairs={{0,1},{1,0},{2,3},{3,2},{4,5},{5,4},{6,7},{7,6},{8,9},{9,8},{10,11... | collective-permute-start | bytes 15728648 | tf_op jit(solution)/shard_map/ppermute | solution.py:28
  44.6 11.2 %collective-permute-start.7 = (f32[32,5120]{1,0:T(8,128)S(1)}, f32[32,5120]{1,0:T(8,128)S(1)}, u32[]{:S(2)}, u32[]{:S(2)}) collective-permute-start(f32[32,5120]{1,0:T(8,128)S(1)} %joined.5.refs_0_.refs_1_), channel_id=1, source_target_pairs={{0,64},{1,9},{4,68},{5,13},{8,72},{9,1},{12,76},{13,5},{32,96},{33... | collective-permute-start | bytes 1966088 | tf_op jit(solution)/shard_map/ppermute | solution.py:38
  47.1 15.9 %collective-permute-start.12 = (f32[640,256]{1,0:T(8,128)S(1)}, f32[640,256]{1,0:T(8,128)S(1)}, u32[]{:S(2)}, u32[]{:S(2)}) collective-permute-start(f32[640,256]{1,0:T(8,128)S(1)} %copy-done.1), channel_id=1, source_target_pairs={{0,1},{1,0},{2,3},{3,2},{4,5},{5,4},{6,7},{7,6},{8,9},{9,8},{10,11... | collective-permute-start | bytes 1966088 | tf_op jit(solution)/shard_map/ppermute | solution.py:28
  47.1 15.9 %collective-permute-start.14 = (f32[640,256]{1,0:T(8,128)S(1)}, f32[640,256]{1,0:T(8,128)S(1)}, u32[]{:S(2)}, u32[]{:S(2)}) collective-permute-start(f32[640,256]{1,0:T(8,128)S(1)} %collective-permute-done.13.refs_2_), channel_id=1, source_target_pairs={{0,1},{1,0},{2,3},{3,2},{4,5},{5,4},{6,7},{7,6},{8,9},{9,8},{10,11... | collective-permute-start | bytes 1966088 | tf_op jit(solution)/shard_map/ppermute | solution.py:28
  47.7 16.4 %collective-permute-start.15 = (f32[128,640]{1,0:T(8,128)S(1)}, f32[128,640]{1,0:T(8,128)S(1)}, u32[]{:S(2)}, u32[]{:S(2)}) collective-permute-start(f32[128,640]{1,0:T(8,128)S(1)} %vir_greens.3.a_ref), channel_id=1, source_target_pairs={{0,2},{2,0},{1,3},{3,1},{4,6},{6,4},{5,7},{7,5},{8,10},{10,8},{9,1... | collective-permute-start | bytes 983048 | tf_op jit(solution)/shard_map/ppermute | solution.py:28
  55.8 7.0 %collective-permute-start.16 = (f32[72,512]{1,0:T(8,128)S(1)}, f32[72,512]{1,0:T(8,128)S(1)}, u32[]{:S(2)}, u32[]{:S(2)}) collective-permute-start(f32[72,512]{1,0:T(8,128)S(1)} %picked.3.here_ref), channel_id=1, source_target_pairs={{0,2},{2,0},{1,3},{3,1},{4,6},{6,4},{5,7},{7,5},{8,10},{10,8},{9,1... | collective-permute-start | bytes 442376 | tf_op jit(solution)/shard_map/ppermute | solution.py:28
  62.8 12.2 %collective-permute-start.10 = (f32[128,640]{1,0:T(8,128)S(1)}, f32[128,640]{1,0:T(8,128)S(1)}, u32[]{:S(2)}, u32[]{:S(2)}) collective-permute-start(f32[128,640]{1,0:T(8,128)S(1)} %vir_greens.2.a_ref), channel_id=1, source_target_pairs={{0,2},{2,0},{1,3},{3,1},{4,6},{6,4},{5,7},{7,5},{8,10},{10,8},{9,1... | collective-permute-start | bytes 983048 | tf_op jit(solution)/shard_map/ppermute | solution.py:28
  66.6 21.3 %collective-permute-start.17 = (f32[64,2048]{1,0:T(8,128)S(1)}, f32[64,2048]{1,0:T(8,128)S(1)}, u32[]{:S(2)}, u32[]{:S(2)}) collective-permute-start(f32[64,2048]{1,0:T(8,128)S(1)} %get-tuple-element.37), channel_id=1, source_target_pairs={{0,32},{1,5},{4,36},{5,9},{8,40},{9,13},{12,44},{13,1},{32,64},{33... | collective-permute-start | bytes 1572872 | tf_op jit(solution)/shard_map/ppermute | solution.py:38
  68.1 6.0 %collective-permute-start.11 = (f32[72,512]{1,0:T(8,128)S(1)}, f32[72,512]{1,0:T(8,128)S(1)}, u32[]{:S(2)}, u32[]{:S(2)}) collective-permute-start(f32[72,512]{1,0:T(8,128)S(1)} %picked.2.here_ref), channel_id=1, source_target_pairs={{0,2},{2,0},{1,3},{3,1},{4,6},{6,4},{5,7},{7,5},{8,10},{10,8},{9,1... | collective-permute-start | bytes 442376 | tf_op jit(solution)/shard_map/ppermute | solution.py:28
  68.9 19.2 %collective-permute-start.19 = (f32[64,2048]{1,0:T(8,128)S(1)}, f32[64,2048]{1,0:T(8,128)S(1)}, u32[]{:S(2)}, u32[]{:S(2)}) collective-permute-start(f32[64,2048]{1,0:T(8,128)S(1)} %get-tuple-element.39), channel_id=1, source_target_pairs={{0,96},{1,13},{4,100},{5,1},{8,104},{9,5},{12,108},{13,9},{32,0},{... | collective-permute-start | bytes 1572872 | tf_op jit(solution)/shard_map/ppermute | solution.py:38
  77.6 10.4 %collective-permute-start.18 = (f32[64,2048]{1,0:T(8,128)S(1)}, f32[64,2048]{1,0:T(8,128)S(1)}, u32[]{:S(2)}, u32[]{:S(2)}) collective-permute-start(f32[64,2048]{1,0:T(8,128)S(1)} %get-tuple-element.38), channel_id=1, source_target_pairs={{0,64},{1,9},{4,68},{5,13},{8,72},{9,1},{12,76},{13,5},{32,96},{33... | collective-permute-start | bytes 1572872 | tf_op jit(solution)/shard_map/ppermute | solution.py:38
  82.6 10.5 %collective-permute-start.25 = (f32[64,2048]{1,0:T(8,128)S(1)}, f32[64,2048]{1,0:T(8,128)S(1)}, u32[]{:S(2)}, u32[]{:S(2)}) collective-permute-start(f32[64,2048]{1,0:T(8,128)S(1)} %get-tuple-element.46), channel_id=1, source_target_pairs={{0,32},{1,5},{4,36},{5,9},{8,40},{9,13},{12,44},{13,1},{32,64},{33... | collective-permute-start | bytes 1572872 | tf_op jit(solution)/shard_map/ppermute | solution.py:38
  83.0 12.9 %collective-permute-start.27 = (f32[64,2048]{1,0:T(8,128)S(1)}, f32[64,2048]{1,0:T(8,128)S(1)}, u32[]{:S(2)}, u32[]{:S(2)}) collective-permute-start(f32[64,2048]{1,0:T(8,128)S(1)} %get-tuple-element.48), channel_id=1, source_target_pairs={{0,96},{1,13},{4,100},{5,1},{8,104},{9,5},{12,108},{13,9},{32,0},{... | collective-permute-start | bytes 1572872 | tf_op jit(solution)/shard_map/ppermute | solution.py:38
  88.0 12.2 %collective-permute-start.26 = (f32[64,2048]{1,0:T(8,128)S(1)}, f32[64,2048]{1,0:T(8,128)S(1)}, u32[]{:S(2)}, u32[]{:S(2)}) collective-permute-start(f32[64,2048]{1,0:T(8,128)S(1)} %get-tuple-element.47), channel_id=1, source_target_pairs={{0,64},{1,9},{4,68},{5,13},{8,72},{9,1},{12,76},{13,5},{32,96},{33... | collective-permute-start | bytes 1572872 | tf_op jit(solution)/shard_map/ppermute | solution.py:38
  88.4 20.4 %collective-permute-start.20 = (f32[16,2048]{1,0:T(8,128)S(1)}, f32[16,2048]{1,0:T(8,128)S(1)}, u32[]{:S(2)}, u32[]{:S(2)}) collective-permute-start(f32[16,2048]{1,0:T(8,128)S(1)} %get-tuple-element.40), channel_id=1, source_target_pairs={{0,0},{1,17},{4,4},{5,21},{8,8},{9,25},{12,12},{13,29},{16,16},{17... | collective-permute-start | bytes 393224 | tf_op jit(solution)/shard_map/ppermute | solution.py:64
  92.5 16.4 %collective-permute-start.21 = (f32[16,2048]{1,0:T(8,128)S(1)}, f32[16,2048]{1,0:T(8,128)S(1)}, u32[]{:S(2)}, u32[]{:S(2)}) collective-permute-start(f32[16,2048]{1,0:T(8,128)S(1)} %get-tuple-element.41), channel_id=1, source_target_pairs={{0,4},{1,49},{4,8},{5,53},{8,12},{9,57},{12,0},{13,61},{16,20},{17... | collective-permute-start | bytes 393224 | tf_op jit(solution)/shard_map/ppermute | solution.py:64
  93.2 16.3 %collective-permute-start.22 = (f32[16,2048]{1,0:T(8,128)S(1)}, f32[16,2048]{1,0:T(8,128)S(1)}, u32[]{:S(2)}, u32[]{:S(2)}) collective-permute-start(f32[16,2048]{1,0:T(8,128)S(1)} %get-tuple-element.42), channel_id=1, source_target_pairs={{0,8},{1,81},{4,12},{5,85},{8,0},{9,89},{12,4},{13,93},{16,24},{17... | collective-permute-start | bytes 393224 | tf_op jit(solution)/shard_map/ppermute | solution.py:64
  95.9 18.2 %collective-permute-start.23 = (f32[16,2048]{1,0:T(8,128)S(1)}, f32[16,2048]{1,0:T(8,128)S(1)}, u32[]{:S(2)}, u32[]{:S(2)}) collective-permute-start(f32[16,2048]{1,0:T(8,128)S(1)} %get-tuple-element.43), channel_id=1, source_target_pairs={{0,12},{1,113},{4,0},{5,117},{8,4},{9,121},{12,8},{13,125},{16,28}... | collective-permute-start | bytes 393224 | tf_op jit(solution)/shard_map/ppermute | solution.py:64
  100.5 13.5 %collective-permute-start.28 = (f32[16,2048]{1,0:T(8,128)S(1)}, f32[16,2048]{1,0:T(8,128)S(1)}, u32[]{:S(2)}, u32[]{:S(2)}) collective-permute-start(f32[16,2048]{1,0:T(8,128)S(1)} %get-tuple-element.49), channel_id=1, source_target_pairs={{0,1},{1,16},{4,5},{5,20},{8,9},{9,24},{12,13},{13,28},{16,17},{17... | collective-permute-start | bytes 393224 | tf_op jit(solution)/shard_map/ppermute | solution.py:64
  108.9 7.3 %collective-permute-start.29 = (f32[16,2048]{1,0:T(8,128)S(1)}, f32[16,2048]{1,0:T(8,128)S(1)}, u32[]{:S(2)}, u32[]{:S(2)}) collective-permute-start(f32[16,2048]{1,0:T(8,128)S(1)} %get-tuple-element.50), channel_id=1, source_target_pairs={{0,5},{1,48},{4,9},{5,52},{8,13},{9,56},{12,1},{13,60},{16,21},{17... | collective-permute-start | bytes 393224 | tf_op jit(solution)/shard_map/ppermute | solution.py:64
  108.9 7.3 %collective-permute-start.30 = (f32[16,2048]{1,0:T(8,128)S(1)}, f32[16,2048]{1,0:T(8,128)S(1)}, u32[]{:S(2)}, u32[]{:S(2)}) collective-permute-start(f32[16,2048]{1,0:T(8,128)S(1)} %get-tuple-element.51), channel_id=1, source_target_pairs={{0,9},{1,80},{4,13},{5,84},{8,1},{9,88},{12,5},{13,92},{16,25},{17... | collective-permute-start | bytes 393224 | tf_op jit(solution)/shard_map/ppermute | solution.py:64
  109.5 6.7 %collective-permute-start.31 = (f32[16,2048]{1,0:T(8,128)S(1)}, f32[16,2048]{1,0:T(8,128)S(1)}, u32[]{:S(2)}, u32[]{:S(2)}) collective-permute-start(f32[16,2048]{1,0:T(8,128)S(1)} %get-tuple-element.52), channel_id=1, source_target_pairs={{0,13},{1,112},{4,1},{5,116},{8,5},{9,120},{12,9},{13,124},{16,29}... | collective-permute-start | bytes 393224 | tf_op jit(solution)/shard_map/ppermute | solution.py:64
  (9 other events, 83.6 us)

commit v2 on v1

--- a/solution.py
+++ b/solution.py
@@ -169,42 +169,25 @@
         ins, w_ref = refs[:n], refs[n]
         sets = refs[n + 1 : n + 5]
         out, stacked = refs[n + 5 :]
-        i = pl.program_id(0)
-
-        @pl.when(i == 0)
-        def _():
-            out[...] = jnp.zeros_like(out)
-
-        for s in range(2):
-
-            @pl.when(i // per == s)
-            def _(s=s):
-                k = pl.multiple_of((i - s * per) * step, 128)
-                w = w_ref[:, pl.ds(s * width + k, step)]
-                for j in range(n):
-                    x = ins[j][:, pl.ds(s * half + occ_count + k, step)]
-                    for t in range(2):
-                        at = (t * n + j) * rows
-                        high, low = parts(x * w[t : t + 1])
-                        stacked[pl.ds(at, rows), :] = high
-                        stacked[pl.ds(total + at, rows), :] = low
-                out[...] += contract_parts(stacked[...], sets[2 * s][...], sets[2 * s + 1][...])
-
-    whole = lambda a: pl.BlockSpec(a.shape, lambda i: (0, 0))
-    return pl.pallas_call(
-        body,
-        grid=(2 * per,),
-        in_specs=[whole(b) for b in blocks]
-        + [whole(weight)]
-        + [
-            pl.BlockSpec((points, step), lambda i: (0, jnp.minimum(i, per - 1))),
-            pl.BlockSpec((points, step), lambda i: (0, jnp.minimum(i, per - 1))),
-            pl.BlockSpec((points, step), lambda i: (0, jnp.maximum(i - per, 0))),
-            pl.BlockSpec((points, step), lambda i: (0, jnp.maximum(i - per, 0))),
-        ],
-        out_specs=pl.BlockSpec((total, points), lambda i: (0, 0)),
+        found = None
+        for i in range(2 * per):
+            s, k = i // per, (i % per) * step
+            for j in range(n):
+                x = ins[j][:, pl.ds(s * half + occ_count + k, step)]
+                for t in range(2):
+                    at = (t * n + j) * rows
+                    high, low = parts(x * w_ref[pl.ds(t, 1), pl.ds(s * width + k, step)])
+                    stacked[i % 2, pl.ds(at, rows), :] = high
+                    stacked[i % 2, pl.ds(total + at, rows), :] = low
+            right = [sets[2 * s + p][:, pl.ds(k, step)] for p in range(2)]
+            part = contract_parts(stacked[i % 2], *right)
+            found = part if found is None else found + part
+        out[...] = found
+
+    return pl.pallas_call(
+        body,
         out_shape=jax.ShapeDtypeStruct((total, points), jnp.float32),
-        scratch_shapes=[pltpu.VMEM((2 * total, step), jnp.bfloat16)],
+        scratch_shapes=[pltpu.VMEM((2, 2 * total, step), jnp.bfloat16)],
         compiler_params=limit(24),
         cost_estimate=pl.CostEstimate(
             flops=6 * total * points * 2 * width, bytes_accessed=14_000_000, transcendentals=0

time: 118 us -> 114 us (0.966)
  Pallas kernels: 27.6 us -> 23.5 us
    pallas_call x2, Pallas kernels: 11.3 us -> 7.18 us  [vir_greens(): pl.pallas_call(body, out_shape=jax.ShapeDtypeStruct((total, points), jnp....]
  transfers between devices with their start and end apart: 32 -> 32, of which waited for: 10 -> 11; matrix products, arithmetic and copies ran while one was open for 1% -> 1% of each run, Pallas kernels for 24% -> 21%
where the time goes in v2:
time: 114 us; the launch traced here: 113 us
  starting transfers between devices  52.6 us (46%)
  waiting for transfers between devices  30.5 us (27%)
  Pallas kernels  23.5 us (21%)
  local copies, waits for them, and re-layouts  4.28 us (4%)
  other arithmetic  1.53 us (1%)
    ppermute x8, starting transfers between devices, to_owner(): return lax.ppermute(x, PTS + ('core',), inner_pairs(by, other))  22.5 us
    ppermute x9, waiting for transfers between devices, outer_shift(): return lax.ppermute(x, ('z', 'x', 'core'), pairs)  19 us
    ppermute x9, starting transfers between devices, outer_shift(): return lax.ppermute(x, ('z', 'x', 'core'), pairs)  13.2 us
    pallas_call x4, Pallas kernels, projections(): pl.pallas_call(body, grid=(count // step,), in_specs=[whole] * 3 + [pl.Bl...  10.3 us
    pallas_call x2, Pallas kernels, vir_greens(): pl.pallas_call(body, out_shape=jax.ShapeDtypeStruct((total, points), jnp....  7.18 us
    ppermute x10, starting transfers between devices, swap(): return lax.ppermute(x, axis, [(0, 1), (1, 0)])  7.18 us
    ppermute x2, waiting for transfers between devices, from_owner(): return lax.ppermute(x, PTS + ('core',), pairs)  5.36 us
    ppermute x2, starting transfers between devices, from_owner(): return lax.ppermute(x, PTS + ('core',), pairs)  5.14 us
  transfers between devices with their start and end apart: 32, of which 11 were waited for; matrix products, arithmetic and copies ran while one was open for 1% of the time, Pallas kernels for 21%

profile of v2, /device:TPU:1, one launch (start us, length us, event | category | flops | bytes accessed | tf_op | source)
XLA Modules:
  0.0 112.8 jit_solution(4099311507191299557)
XLA Ops:
  0.0 1.4 %collective-permute-start.9 = (f32[640,2304]{1,0:T(8,128)}, f32[640,2304]{1,0:T(8,128)S(1)}, u32[]{:S(2)}, u32[]{:S(2)}) collective-permute-start(f32[640,2304]{1,0:T(8,128)} %ref.1), channel_id=1, source_target_pairs={{0,1},{1,0},{2,3},{3,2},{4,5},{5,4},{6,7},{7,6},{8,9},{9,8},{10,11... | collective-permute-start | bytes 17694728 | tf_op jit(solution)/shard_map/ppermute | solution.py:28
  3.0 5.1 %collective-permute-start = (f32[8,2560]{1,0:T(8,128)S(1)}, f32[8,2560]{1,0:T(8,128)S(1)}, u32[]{:S(2)}, u32[]{:S(2)}) collective-permute-start(f32[8,2560]{1,0:T(8,128)S(1)} %joined.3), channel_id=1, source_target_pairs={{0,0},{17,1},{4,4},{21,5},{8,8},{25,9},{12,12},{29,13},{16,16},{1,... | collective-permute-start | bytes 245768 | tf_op jit(solution)/shard_map/ppermute | solution.py:69
  8.1 1.7 %collective-permute-done.refs_0_ = f32[8,2560]{1,0:T(8,128)S(1)} collective-permute-done((f32[8,2560]{1,0:T(8,128)S(1)}, f32[8,2560]{1,0:T(8,128)S(1)}, u32[]{:S(2)}, u32[]{:S(2)}) %collective-permute-start) | collective-permute-done | bytes 81952 | tf_op jit(solution)/shard_map/ppermute | solution.py:69
  9.9 3.6 %collective-permute-done.1.refs_1_ = f32[8,2560]{1,0:T(8,128)S(1)} collective-permute-done((f32[8,2560]{1,0:T(8,128)S(1)}, f32[8,2560]{1,0:T(8,128)S(1)}, u32[]{:S(2)}, u32[]{:S(2)}) %collective-permute-start.1) | collective-permute-done | bytes 81952 | tf_op jit(solution)/shard_map/ppermute | solution.py:69
  13.5 3.8 %collective-permute-start.2 = (f32[8,5120]{1,0:T(8,128)S(1)}, f32[8,5120]{1,0:T(8,128)S(1)}, u32[]{:S(2)}, u32[]{:S(2)}) collective-permute-start(f32[8,5120]{1,0:T(8,128)S(1)} %joined.4.refs_0_), channel_id=1, source_target_pairs={{0,12},{1,97},{4,0},{5,101},{8,4},{9,105},{12,8},{13,109},{32,44},... | collective-permute-start | bytes 491528 | tf_op jit(solution)/shard_map/ppermute | solution.py:48
  18.8 2.7 %copy-done = f32[640,2304]{1,0:T(8,128)S(1)} copy-done((f32[640,2304]{1,0:T(8,128)S(1)}, f32[640,2304]{1,0:T(8,128)}, u32[]{:S(2)}) %copy-start) | copy-done | bytes 5898264
  21.4 1.6 %split.2 = (bf16[640,2304]{1,0:T(8,128)(2,1)S(1)}, bf16[640,2304]{1,0:T(8,128)(2,1)S(1)}) custom-call(f32[640,2304]{1,0:T(8,128)S(1)} %copy-done), custom_call_target="tpu_custom_call" | custom-call | tf_op jit(solution)/shard_map/split/pallas_call | solution.py:141
  24.5 2.5 %collective-permute-start.5 = (f32[32,5120]{1,0:T(8,128)S(1)}, f32[32,5120]{1,0:T(8,128)S(1)}, u32[]{:S(2)}, u32[]{:S(2)}) collective-permute-start(f32[32,5120]{1,0:T(8,128)S(1)} %joined.5.refs_0_.refs_1_), channel_id=1, source_target_pairs={{0,96},{1,13},{4,100},{5,1},{8,104},{9,5},{12,108},{13,9},{32,0},{... | collective-permute-start | bytes 1966088 | tf_op jit(solution)/shard_map/ppermute | solution.py:38
  27.2 1.7 %split.3 = (bf16[640,2304]{1,0:T(8,128)(2,1)S(1)}, bf16[640,2304]{1,0:T(8,128)(2,1)S(1)}) custom-call(f32[640,2304]{1,0:T(8,128)S(1)} %collective-permute-done.9.ref), custom_call_target="tpu_custom_call" | custom-call | tf_op jit(solution)/shard_map/split/pallas_call | solution.py:141
  28.9 5.7 %collective-permute-done.5.refs_0_.refs_1_ = f32[32,5120]{1,0:T(8,128)S(1)} collective-permute-done((f32[32,5120]{1,0:T(8,128)S(1)}, f32[32,5120]{1,0:T(8,128)S(1)}, u32[]{:S(2)}, u32[]{:S(2)}) %collective-permute-start.5) | collective-permute-done | bytes 655392 | tf_op jit(solution)/shard_map/ppermute | solution.py:38
  34.6 3.4 %collective-permute-done.6.refs_1_.refs_2_.refs_3_ = f32[32,5120]{1,0:T(8,128)S(1)} collective-permute-done((f32[32,5120]{1,0:T(8,128)S(1)}, f32[32,5120]{1,0:T(8,128)S(1)}, u32[]{:S(2)}, u32[]{:S(2)}) %collective-permute-start.6) | collective-permute-done | bytes 655392 | tf_op jit(solution)/shard_map/ppermute | solution.py:38
  38.0 3.6 %vir_greens.3.a_ref = f32[128,640]{1,0:T(8,128)S(1)} custom-call(f32[32,5120]{1,0:T(8,128)S(1)} %collective-permute-done.5.refs_0_.refs_1_, f32[32,5120]{1,0:T(8,128)S(1)} %collective-permute-done.6.refs_1_.refs_2_.refs_3_, f32[2,4608]{1,0:T(2,128)S(1)} %multiply_exponential_fusion.refs_2_, bf16[640,2304]{1,0:T(8,128)(2,1)S(1)} %get-tuple-element.30.refs_3_, ...), custom_call_target="tpu_custom_call" | custom-call | flops 2264924160 | bytes 14000000 | tf_op jit(solution)/shard_map/vir_greens/pallas_call | solution.py:187
  42.5 2.5 %collective-permute-start.7 = (f32[32,5120]{1,0:T(8,128)S(1)}, f32[32,5120]{1,0:T(8,128)S(1)}, u32[]{:S(2)}, u32[]{:S(2)}) collective-permute-start(f32[32,5120]{1,0:T(8,128)S(1)} %joined.5.refs_0_.refs_1_), channel_id=1, source_target_pairs={{0,64},{1,9},{4,68},{5,13},{8,72},{9,1},{12,76},{13,5},{32,96},{33... | collective-permute-start | bytes 1966088 | tf_op jit(solution)/shard_map/ppermute | solution.py:38
  46.7 7.1 %collective-permute-done.7.refs_1_.refs_2_.refs_3_ = f32[32,5120]{1,0:T(8,128)S(1)} collective-permute-done((f32[32,5120]{1,0:T(8,128)S(1)}, f32[32,5120]{1,0:T(8,128)S(1)}, u32[]{:S(2)}, u32[]{:S(2)}) %collective-permute-start.7) | collective-permute-done | bytes 655392 | tf_op jit(solution)/shard_map/ppermute | solution.py:38
  53.7 1.3 %collective-permute-start.16 = (f32[72,512]{1,0:T(8,128)S(1)}, f32[72,512]{1,0:T(8,128)S(1)}, u32[]{:S(2)}, u32[]{:S(2)}) collective-permute-start(f32[72,512]{1,0:T(8,128)S(1)} %picked.3.here_ref), channel_id=1, source_target_pairs={{0,2},{2,0},{1,3},{3,1},{4,6},{6,4},{5,7},{7,5},{8,10},{10,8},{9,1... | collective-permute-start | bytes 442376 | tf_op jit(solution)/shard_map/ppermute | solution.py:28
  55.0 3.6 %vir_greens.2.a_ref = f32[128,640]{1,0:T(8,128)S(1)} custom-call(f32[32,5120]{1,0:T(8,128)S(1)} %joined.5.refs_0_.refs_1_, f32[32,5120]{1,0:T(8,128)S(1)} %collective-permute-done.7.refs_1_.refs_2_.refs_3_, f32[2,4608]{1,0:T(2,128)S(1)} %multiply_exponential_fusion.refs_2_, bf16[640,2304]{1,0:T(8,128)(2,1)S(1)} %get-tuple-element.30.refs_3_, ...), custom_call_target="tpu_custom_call" | custom-call | flops 2264924160 | bytes 14000000 | tf_op jit(solution)/shard_map/vir_greens/pallas_call | solution.py:187
  60.5 2.6 %projections.5 = (f32[64,2048]{1,0:T(8,128)S(1)}, f32[64,2048]{1,0:T(8,128)S(1)}) custom-call(f32[128,640]{1,0:T(8,128)S(1)} %vir_greens.3.a_ref, f32[128,640]{1,0:T(8,128)S(1)} %collective-permute-done.15.b_ref, f32[128,640]{1,0:T(8,128)S(1)} %occ_greens.3.o_ref, f32[2048,640]{1,0:T(8,128)S(1)} %bitcast.5), custom_call_target="tpu_custom_call" | custom-call | flops 1006632960 | bytes 8000000 | tf_op jit(solution)/shard_map/projections/pallas_call | solution.py:256
  63.1 1.1 collective-permute-start.17
  64.9 1.9 %collective-permute-start.19 = (f32[64,2048]{1,0:T(8,128)S(1)}, f32[64,2048]{1,0:T(8,128)S(1)}, u32[]{:S(2)}, u32[]{:S(2)}) collective-permute-start(f32[64,2048]{1,0:T(8,128)S(1)} %get-tuple-element.39), channel_id=1, source_target_pairs={{0,96},{1,13},{4,100},{5,1},{8,104},{9,5},{12,108},{13,9},{32,0},{... | collective-permute-start | bytes 1572872 | tf_op jit(solution)/shard_map/ppermute | solution.py:38
  66.8 3.3 %collective-permute-done.11.there_ref = f32[72,512]{1,0:T(8,128)S(1)} collective-permute-done((f32[72,512]{1,0:T(8,128)S(1)}, f32[72,512]{1,0:T(8,128)S(1)}, u32[]{:S(2)}, u32[]{:S(2)}) %collective-permute-start.11) | collective-permute-done | bytes 147488 | tf_op jit(solution)/shard_map/ppermute | solution.py:28
  71.1 2.6 %projections.4 = (f32[64,2048]{1,0:T(8,128)S(1)}, f32[64,2048]{1,0:T(8,128)S(1)}) custom-call(f32[128,640]{1,0:T(8,128)S(1)} %vir_greens.2.a_ref, f32[128,640]{1,0:T(8,128)S(1)} %collective-permute-done.10.b_ref, f32[128,640]{1,0:T(8,128)S(1)} %occ_greens.2.o_ref, f32[2048,640]{1,0:T(8,128)S(1)} %bitcast.5), custom_call_target="tpu_custom_call" | custom-call | flops 1006632960 | bytes 8000000 | tf_op jit(solution)/shard_map/projections/pallas_call | solution.py:256
  73.7 2.3 %collective-permute-start.18 = (f32[64,2048]{1,0:T(8,128)S(1)}, f32[64,2048]{1,0:T(8,128)S(1)}, u32[]{:S(2)}, u32[]{:S(2)}) collective-permute-start(f32[64,2048]{1,0:T(8,128)S(1)} %get-tuple-element.38), channel_id=1, source_target_pairs={{0,64},{1,9},{4,68},{5,13},{8,72},{9,1},{12,76},{13,5},{32,96},{33... | collective-permute-start | bytes 1572872 | tf_op jit(solution)/shard_map/ppermute | solution.py:38
  76.0 2.6 %projections.7 = (f32[64,2048]{1,0:T(8,128)S(1)}, f32[64,2048]{1,0:T(8,128)S(1)}) custom-call(f32[128,640]{1,0:T(8,128)S(1)} %vir_greens.3.a_ref, f32[128,640]{1,0:T(8,128)S(1)} %collective-permute-done.15.b_ref, f32[128,640]{1,0:T(8,128)S(1)} %occ_greens.3.o_ref, f32[2048,640]{1,0:T(8,128)S(1)} %collective-permute-done.24.w_ref), custom_call_target="tpu_custom_call" | custom-call | flops 1006632960 | bytes 8000000 | tf_op jit(solution)/shard_map/projections/pallas_call | solution.py:256
  78.9 2.4 %collective-permute-start.27 = (f32[64,2048]{1,0:T(8,128)S(1)}, f32[64,2048]{1,0:T(8,128)S(1)}, u32[]{:S(2)}, u32[]{:S(2)}) collective-permute-start(f32[64,2048]{1,0:T(8,128)S(1)} %get-tuple-element.48), channel_id=1, source_target_pairs={{0,96},{1,13},{4,100},{5,1},{8,104},{9,5},{12,108},{13,9},{32,0},{... | collective-permute-start | bytes 1572872 | tf_op jit(solution)/shard_map/ppermute | solution.py:38
  81.3 2.6 %projections.6 = (f32[64,2048]{1,0:T(8,128)S(1)}, f32[64,2048]{1,0:T(8,128)S(1)}) custom-call(f32[128,640]{1,0:T(8,128)S(1)} %vir_greens.2.a_ref, f32[128,640]{1,0:T(8,128)S(1)} %collective-permute-done.10.b_ref, f32[128,640]{1,0:T(8,128)S(1)} %occ_greens.2.o_ref, f32[2048,640]{1,0:T(8,128)S(1)} %collective-permute-done.24.w_ref), custom_call_target="tpu_custom_call" | custom-call | flops 1006632960 | bytes 8000000 | tf_op jit(solution)/shard_map/projections/pallas_call | solution.py:256
  84.4 4.1 %collective-permute-start.20 = (f32[16,2048]{1,0:T(8,128)S(1)}, f32[16,2048]{1,0:T(8,128)S(1)}, u32[]{:S(2)}, u32[]{:S(2)}) collective-permute-start(f32[16,2048]{1,0:T(8,128)S(1)} %get-tuple-element.40), channel_id=1, source_target_pairs={{0,0},{1,17},{4,4},{5,21},{8,8},{9,25},{12,12},{13,29},{16,16},{17... | collective-permute-start | bytes 393224 | tf_op jit(solution)/shard_map/ppermute | solution.py:64
  89.2 2.9 %collective-permute-start.22 = (f32[16,2048]{1,0:T(8,128)S(1)}, f32[16,2048]{1,0:T(8,128)S(1)}, u32[]{:S(2)}, u32[]{:S(2)}) collective-permute-start(f32[16,2048]{1,0:T(8,128)S(1)} %get-tuple-element.42), channel_id=1, source_target_pairs={{0,8},{1,81},{4,12},{5,85},{8,0},{9,89},{12,4},{13,93},{16,24},{17... | collective-permute-start | bytes 393224 | tf_op jit(solution)/shard_map/ppermute | solution.py:64
  92.1 2.0 %collective-permute-start.23 = (f32[16,2048]{1,0:T(8,128)S(1)}, f32[16,2048]{1,0:T(8,128)S(1)}, u32[]{:S(2)}, u32[]{:S(2)}) collective-permute-start(f32[16,2048]{1,0:T(8,128)S(1)} %get-tuple-element.43), channel_id=1, source_target_pairs={{0,12},{1,113},{4,0},{5,117},{8,4},{9,121},{12,8},{13,125},{16,28}... | collective-permute-start | bytes 393224 | tf_op jit(solution)/shard_map/ppermute | solution.py:64
  94.1 2.1 %collective-permute-done.26.refs_2_ = f32[64,2048]{1,0:T(8,128)S(1)} collective-permute-done((f32[64,2048]{1,0:T(8,128)S(1)}, f32[64,2048]{1,0:T(8,128)S(1)}, u32[]{:S(2)}, u32[]{:S(2)}) %collective-permute-start.26) | collective-permute-done | bytes 524320 | tf_op jit(solution)/shard_map/ppermute | solution.py:38
  96.6 8.2 %collective-permute-start.28 = (f32[16,2048]{1,0:T(8,128)S(1)}, f32[16,2048]{1,0:T(8,128)S(1)}, u32[]{:S(2)}, u32[]{:S(2)}) collective-permute-start(f32[16,2048]{1,0:T(8,128)S(1)} %get-tuple-element.49), channel_id=1, source_target_pairs={{0,1},{1,16},{4,5},{5,20},{8,9},{9,24},{12,13},{13,28},{16,17},{17... | collective-permute-start | bytes 393224 | tf_op jit(solution)/shard_map/ppermute | solution.py:64
  105.2 4.9 %collective-permute-start.31 = (f32[16,2048]{1,0:T(8,128)S(1)}, f32[16,2048]{1,0:T(8,128)S(1)}, u32[]{:S(2)}, u32[]{:S(2)}) collective-permute-start(f32[16,2048]{1,0:T(8,128)S(1)} %get-tuple-element.52), channel_id=1, source_target_pairs={{0,13},{1,112},{4,1},{5,116},{8,5},{9,120},{12,9},{13,124},{16,29}... | collective-permute-start | bytes 393224 | tf_op jit(solution)/shard_map/ppermute | solution.py:64
  110.4 1.6 %collective-permute-done.30 = f32[16,2048]{1,0:T(8,128)S(1)} collective-permute-done((f32[16,2048]{1,0:T(8,128)S(1)}, f32[16,2048]{1,0:T(8,128)S(1)}, u32[]{:S(2)}, u32[]{:S(2)}) %collective-permute-start.30) | collective-permute-done | bytes 131104 | tf_op jit(solution)/shard_map/ppermute | solution.py:64
  (76 shorter events, 13.9 us)
Async XLA Ops:
  0.0 27.2 %collective-permute-start.9 = (f32[640,2304]{1,0:T(8,128)}, f32[640,2304]{1,0:T(8,128)S(1)}, u32[]{:S(2)}, u32[]{:S(2)}) collective-permute-start(f32[640,2304]{1,0:T(8,128)} %ref.1), channel_id=1, source_target_pairs={{0,1},{1,0},{2,3},{3,2},{4,5},{5,4},{6,7},{7,6},{8,9},{9,8},{10,11... | collective-permute-start | bytes 17694728 | tf_op jit(solution)/shard_map/ppermute | solution.py:28
  3.0 6.9 %collective-permute-start = (f32[8,2560]{1,0:T(8,128)S(1)}, f32[8,2560]{1,0:T(8,128)S(1)}, u32[]{:S(2)}, u32[]{:S(2)}) collective-permute-start(f32[8,2560]{1,0:T(8,128)S(1)} %joined.3), channel_id=1, source_target_pairs={{0,0},{17,1},{4,4},{21,5},{8,8},{25,9},{12,12},{29,13},{16,16},{1,... | collective-permute-start | bytes 245768 | tf_op jit(solution)/shard_map/ppermute | solution.py:69
  8.1 5.4 %collective-permute-start.1 = (f32[8,2560]{1,0:T(8,128)S(1)}, f32[8,2560]{1,0:T(8,128)S(1)}, u32[]{:S(2)}, u32[]{:S(2)}) collective-permute-start(f32[8,2560]{1,0:T(8,128)S(1)} %joined.3), channel_id=1, source_target_pairs={{1,0},{16,1},{5,4},{20,5},{9,8},{24,9},{13,12},{28,13},{17,16},{0,... | collective-permute-start | bytes 245768 | tf_op jit(solution)/shard_map/ppermute | solution.py:69
  13.5 10.1 %collective-permute-start.2 = (f32[8,5120]{1,0:T(8,128)S(1)}, f32[8,5120]{1,0:T(8,128)S(1)}, u32[]{:S(2)}, u32[]{:S(2)}) collective-permute-start(f32[8,5120]{1,0:T(8,128)S(1)} %joined.4.refs_0_), channel_id=1, source_target_pairs={{0,12},{1,97},{4,0},{5,101},{8,4},{9,105},{12,8},{13,109},{32,44},... | collective-permute-start | bytes 491528 | tf_op jit(solution)/shard_map/ppermute | solution.py:48
  17.3 6.3 %collective-permute-start.3 = (f32[8,5120]{1,0:T(8,128)S(1)}, f32[8,5120]{1,0:T(8,128)S(1)}, u32[]{:S(2)}, u32[]{:S(2)}) collective-permute-start(f32[8,5120]{1,0:T(8,128)S(1)} %joined.4.refs_0_), channel_id=1, source_target_pairs={{0,8},{1,65},{4,12},{5,69},{8,0},{9,73},{12,4},{13,77},{32,40},{33... | collective-permute-start | bytes 491528 | tf_op jit(solution)/shard_map/ppermute | solution.py:48
  17.3 7.1 %collective-permute-start.4 = (f32[8,5120]{1,0:T(8,128)S(1)}, f32[8,5120]{1,0:T(8,128)S(1)}, u32[]{:S(2)}, u32[]{:S(2)}) collective-permute-start(f32[8,5120]{1,0:T(8,128)S(1)} %joined.4.refs_0_), channel_id=1, source_target_pairs={{0,4},{1,33},{4,8},{5,37},{8,12},{9,41},{12,0},{13,45},{32,36},{33... | collective-permute-start | bytes 491528 | tf_op jit(solution)/shard_map/ppermute | solution.py:48
  18.8 4.3 %collective-permute-start.8 = (f32[2560]{0:T(1024)S(1)}, f32[2560]{0:T(1024)S(1)}, u32[]{:S(2)}, u32[]{:S(2)}) collective-permute-start(f32[2560]{0:T(1024)S(1)} %pad_maximum_fusion.1), channel_id=1, source_target_pairs={{0,1},{1,0},{2,3},{3,2},{4,5},{5,4},{6,7},{7,6},{8,9},{9,8},{10,11... | collective-permute-start | bytes 30728 | tf_op jit(solution)/shard_map/ppermute | solution.py:28
  23.1 18.5 %collective-permute-start.13 = (f32[640,256]{1,0:T(8,128)S(1)}, f32[640,256]{1,0:T(8,128)S(1)}, u32[]{:S(2)}, u32[]{:S(2)}) collective-permute-start(f32[640,256]{1,0:T(8,128)S(1)} %copy-done.1), channel_id=1, source_target_pairs={{0,2},{2,0},{1,3},{3,1},{4,6},{6,4},{5,7},{7,5},{8,10},{10,8},{9,1... | collective-permute-start | bytes 1966088 | tf_op jit(solution)/shard_map/ppermute | solution.py:28
  24.5 10.1 %collective-permute-start.5 = (f32[32,5120]{1,0:T(8,128)S(1)}, f32[32,5120]{1,0:T(8,128)S(1)}, u32[]{:S(2)}, u32[]{:S(2)}) collective-permute-start(f32[32,5120]{1,0:T(8,128)S(1)} %joined.5.refs_0_.refs_1_), channel_id=1, source_target_pairs={{0,96},{1,13},{4,100},{5,1},{8,104},{9,5},{12,108},{13,9},{32,0},{... | collective-permute-start | bytes 1966088 | tf_op jit(solution)/shard_map/ppermute | solution.py:38
  27.1 10.9 %collective-permute-start.6 = (f32[32,5120]{1,0:T(8,128)S(1)}, f32[32,5120]{1,0:T(8,128)S(1)}, u32[]{:S(2)}, u32[]{:S(2)}) collective-permute-start(f32[32,5120]{1,0:T(8,128)S(1)} %joined.5.refs_0_.refs_1_), channel_id=1, source_target_pairs={{0,32},{1,5},{4,36},{5,9},{8,40},{9,13},{12,44},{13,1},{32,64},{33... | collective-permute-start | bytes 1966088 | tf_op jit(solution)/shard_map/ppermute | solution.py:38
  41.7 34.4 %collective-permute-start.24 = (f32[2048,640]{1,0:T(8,128)S(1)}, f32[2048,640]{1,0:T(8,128)S(1)}, u32[]{:S(2)}, u32[]{:S(2)}) collective-permute-start(f32[2048,640]{1,0:T(8,128)S(1)} %bitcast.5), channel_id=1, source_target_pairs={{0,1},{1,0},{2,3},{3,2},{4,5},{5,4},{6,7},{7,6},{8,9},{9,8},{10,11... | collective-permute-start | bytes 15728648 | tf_op jit(solution)/shard_map/ppermute | solution.py:28
  42.5 11.2 %collective-permute-start.7 = (f32[32,5120]{1,0:T(8,128)S(1)}, f32[32,5120]{1,0:T(8,128)S(1)}, u32[]{:S(2)}, u32[]{:S(2)}) collective-permute-start(f32[32,5120]{1,0:T(8,128)S(1)} %joined.5.refs_0_.refs_1_), channel_id=1, source_target_pairs={{0,64},{1,9},{4,68},{5,13},{8,72},{9,1},{12,76},{13,5},{32,96},{33... | collective-permute-start | bytes 1966088 | tf_op jit(solution)/shard_map/ppermute | solution.py:38
  45.1 14.4 %collective-permute-start.12 = (f32[640,256]{1,0:T(8,128)S(1)}, f32[640,256]{1,0:T(8,128)S(1)}, u32[]{:S(2)}, u32[]{:S(2)}) collective-permute-start(f32[640,256]{1,0:T(8,128)S(1)} %copy-done.1), channel_id=1, source_target_pairs={{0,1},{1,0},{2,3},{3,2},{4,5},{5,4},{6,7},{7,6},{8,9},{9,8},{10,11... | collective-permute-start | bytes 1966088 | tf_op jit(solution)/shard_map/ppermute | solution.py:28
  45.1 14.4 %collective-permute-start.14 = (f32[640,256]{1,0:T(8,128)S(1)}, f32[640,256]{1,0:T(8,128)S(1)}, u32[]{:S(2)}, u32[]{:S(2)}) collective-permute-start(f32[640,256]{1,0:T(8,128)S(1)} %collective-permute-done.13.refs_2_), channel_id=1, source_target_pairs={{0,1},{1,0},{2,3},{3,2},{4,5},{5,4},{6,7},{7,6},{8,9},{9,8},{10,11... | collective-permute-start | bytes 1966088 | tf_op jit(solution)/shard_map/ppermute | solution.py:28
  45.6 14.9 %collective-permute-start.15 = (f32[128,640]{1,0:T(8,128)S(1)}, f32[128,640]{1,0:T(8,128)S(1)}, u32[]{:S(2)}, u32[]{:S(2)}) collective-permute-start(f32[128,640]{1,0:T(8,128)S(1)} %vir_greens.3.a_ref), channel_id=1, source_target_pairs={{0,2},{2,0},{1,3},{3,1},{4,6},{6,4},{5,7},{7,5},{8,10},{10,8},{9,1... | collective-permute-start | bytes 983048 | tf_op jit(solution)/shard_map/ppermute | solution.py:28
  53.7 4.9 %collective-permute-start.16 = (f32[72,512]{1,0:T(8,128)S(1)}, f32[72,512]{1,0:T(8,128)S(1)}, u32[]{:S(2)}, u32[]{:S(2)}) collective-permute-start(f32[72,512]{1,0:T(8,128)S(1)} %picked.3.here_ref), channel_id=1, source_target_pairs={{0,2},{2,0},{1,3},{3,1},{4,6},{6,4},{5,7},{7,5},{8,10},{10,8},{9,1... | collective-permute-start | bytes 442376 | tf_op jit(solution)/shard_map/ppermute | solution.py:28
  58.6 12.4 %collective-permute-start.10 = (f32[128,640]{1,0:T(8,128)S(1)}, f32[128,640]{1,0:T(8,128)S(1)}, u32[]{:S(2)}, u32[]{:S(2)}) collective-permute-start(f32[128,640]{1,0:T(8,128)S(1)} %vir_greens.2.a_ref), channel_id=1, source_target_pairs={{0,2},{2,0},{1,3},{3,1},{4,6},{6,4},{5,7},{7,5},{8,10},{10,8},{9,1... | collective-permute-start | bytes 983048 | tf_op jit(solution)/shard_map/ppermute | solution.py:28
  63.1 20.9 %collective-permute-start.17 = (f32[64,2048]{1,0:T(8,128)S(1)}, f32[64,2048]{1,0:T(8,128)S(1)}, u32[]{:S(2)}, u32[]{:S(2)}) collective-permute-start(f32[64,2048]{1,0:T(8,128)S(1)} %get-tuple-element.37), channel_id=1, source_target_pairs={{0,32},{1,5},{4,36},{5,9},{8,40},{9,13},{12,44},{13,1},{32,64},{33... | collective-permute-start | bytes 1572872 | tf_op jit(solution)/shard_map/ppermute | solution.py:38
  64.2 6.0 %collective-permute-start.11 = (f32[72,512]{1,0:T(8,128)S(1)}, f32[72,512]{1,0:T(8,128)S(1)}, u32[]{:S(2)}, u32[]{:S(2)}) collective-permute-start(f32[72,512]{1,0:T(8,128)S(1)} %picked.2.here_ref), channel_id=1, source_target_pairs={{0,2},{2,0},{1,3},{3,1},{4,6},{6,4},{5,7},{7,5},{8,10},{10,8},{9,1... | collective-permute-start | bytes 442376 | tf_op jit(solution)/shard_map/ppermute | solution.py:28
  64.9 19.1 %collective-permute-start.19 = (f32[64,2048]{1,0:T(8,128)S(1)}, f32[64,2048]{1,0:T(8,128)S(1)}, u32[]{:S(2)}, u32[]{:S(2)}) collective-permute-start(f32[64,2048]{1,0:T(8,128)S(1)} %get-tuple-element.39), channel_id=1, source_target_pairs={{0,96},{1,13},{4,100},{5,1},{8,104},{9,5},{12,108},{13,9},{32,0},{... | collective-permute-start | bytes 1572872 | tf_op jit(solution)/shard_map/ppermute | solution.py:38
  73.7 10.4 %collective-permute-start.18 = (f32[64,2048]{1,0:T(8,128)S(1)}, f32[64,2048]{1,0:T(8,128)S(1)}, u32[]{:S(2)}, u32[]{:S(2)}) collective-permute-start(f32[64,2048]{1,0:T(8,128)S(1)} %get-tuple-element.38), channel_id=1, source_target_pairs={{0,64},{1,9},{4,68},{5,13},{8,72},{9,1},{12,76},{13,5},{32,96},{33... | collective-permute-start | bytes 1572872 | tf_op jit(solution)/shard_map/ppermute | solution.py:38
  78.6 10.6 %collective-permute-start.25 = (f32[64,2048]{1,0:T(8,128)S(1)}, f32[64,2048]{1,0:T(8,128)S(1)}, u32[]{:S(2)}, u32[]{:S(2)}) collective-permute-start(f32[64,2048]{1,0:T(8,128)S(1)} %get-tuple-element.46), channel_id=1, source_target_pairs={{0,32},{1,5},{4,36},{5,9},{8,40},{9,13},{12,44},{13,1},{32,64},{33... | collective-permute-start | bytes 1572872 | tf_op jit(solution)/shard_map/ppermute | solution.py:38
  78.9 13.1 %collective-permute-start.27 = (f32[64,2048]{1,0:T(8,128)S(1)}, f32[64,2048]{1,0:T(8,128)S(1)}, u32[]{:S(2)}, u32[]{:S(2)}) collective-permute-start(f32[64,2048]{1,0:T(8,128)S(1)} %get-tuple-element.48), channel_id=1, source_target_pairs={{0,96},{1,13},{4,100},{5,1},{8,104},{9,5},{12,108},{13,9},{32,0},{... | collective-permute-start | bytes 1572872 | tf_op jit(solution)/shard_map/ppermute | solution.py:38
  83.9 12.3 %collective-permute-start.26 = (f32[64,2048]{1,0:T(8,128)S(1)}, f32[64,2048]{1,0:T(8,128)S(1)}, u32[]{:S(2)}, u32[]{:S(2)}) collective-permute-start(f32[64,2048]{1,0:T(8,128)S(1)} %get-tuple-element.47), channel_id=1, source_target_pairs={{0,64},{1,9},{4,68},{5,13},{8,72},{9,1},{12,76},{13,5},{32,96},{33... | collective-permute-start | bytes 1572872 | tf_op jit(solution)/shard_map/ppermute | solution.py:38
  84.4 20.4 %collective-permute-start.20 = (f32[16,2048]{1,0:T(8,128)S(1)}, f32[16,2048]{1,0:T(8,128)S(1)}, u32[]{:S(2)}, u32[]{:S(2)}) collective-permute-start(f32[16,2048]{1,0:T(8,128)S(1)} %get-tuple-element.40), channel_id=1, source_target_pairs={{0,0},{1,17},{4,4},{5,21},{8,8},{9,25},{12,12},{13,29},{16,16},{17... | collective-permute-start | bytes 393224 | tf_op jit(solution)/shard_map/ppermute | solution.py:64
  88.5 16.3 %collective-permute-start.21 = (f32[16,2048]{1,0:T(8,128)S(1)}, f32[16,2048]{1,0:T(8,128)S(1)}, u32[]{:S(2)}, u32[]{:S(2)}) collective-permute-start(f32[16,2048]{1,0:T(8,128)S(1)} %get-tuple-element.41), channel_id=1, source_target_pairs={{0,4},{1,49},{4,8},{5,53},{8,12},{9,57},{12,0},{13,61},{16,20},{17... | collective-permute-start | bytes 393224 | tf_op jit(solution)/shard_map/ppermute | solution.py:64
  89.2 16.0 %collective-permute-start.22 = (f32[16,2048]{1,0:T(8,128)S(1)}, f32[16,2048]{1,0:T(8,128)S(1)}, u32[]{:S(2)}, u32[]{:S(2)}) collective-permute-start(f32[16,2048]{1,0:T(8,128)S(1)} %get-tuple-element.42), channel_id=1, source_target_pairs={{0,8},{1,81},{4,12},{5,85},{8,0},{9,89},{12,4},{13,93},{16,24},{17... | collective-permute-start | bytes 393224 | tf_op jit(solution)/shard_map/ppermute | solution.py:64
  92.1 18.0 %collective-permute-start.23 = (f32[16,2048]{1,0:T(8,128)S(1)}, f32[16,2048]{1,0:T(8,128)S(1)}, u32[]{:S(2)}, u32[]{:S(2)}) collective-permute-start(f32[16,2048]{1,0:T(8,128)S(1)} %get-tuple-element.43), channel_id=1, source_target_pairs={{0,12},{1,113},{4,0},{5,117},{8,4},{9,121},{12,8},{13,125},{16,28}... | collective-permute-start | bytes 393224 | tf_op jit(solution)/shard_map/ppermute | solution.py:64
  96.6 13.5 %collective-permute-start.28 = (f32[16,2048]{1,0:T(8,128)S(1)}, f32[16,2048]{1,0:T(8,128)S(1)}, u32[]{:S(2)}, u32[]{:S(2)}) collective-permute-start(f32[16,2048]{1,0:T(8,128)S(1)} %get-tuple-element.49), channel_id=1, source_target_pairs={{0,1},{1,16},{4,5},{5,20},{8,9},{9,24},{12,13},{13,28},{16,17},{17... | collective-permute-start | bytes 393224 | tf_op jit(solution)/shard_map/ppermute | solution.py:64
  104.8 5.6 %collective-permute-start.29 = (f32[16,2048]{1,0:T(8,128)S(1)}, f32[16,2048]{1,0:T(8,128)S(1)}, u32[]{:S(2)}, u32[]{:S(2)}) collective-permute-start(f32[16,2048]{1,0:T(8,128)S(1)} %get-tuple-element.50), channel_id=1, source_target_pairs={{0,5},{1,48},{4,9},{5,52},{8,13},{9,56},{12,1},{13,60},{16,21},{17... | collective-permute-start | bytes 393224 | tf_op jit(solution)/shard_map/ppermute | solution.py:64
  104.8 7.2 %collective-permute-start.30 = (f32[16,2048]{1,0:T(8,128)S(1)}, f32[16,2048]{1,0:T(8,128)S(1)}, u32[]{:S(2)}, u32[]{:S(2)}) collective-permute-start(f32[16,2048]{1,0:T(8,128)S(1)} %get-tuple-element.51), channel_id=1, source_target_pairs={{0,9},{1,80},{4,13},{5,84},{8,1},{9,88},{12,5},{13,92},{16,25},{17... | collective-permute-start | bytes 393224 | tf_op jit(solution)/shard_map/ppermute | solution.py:64
  105.2 6.8 %collective-permute-start.31 = (f32[16,2048]{1,0:T(8,128)S(1)}, f32[16,2048]{1,0:T(8,128)S(1)}, u32[]{:S(2)}, u32[]{:S(2)}) collective-permute-start(f32[16,2048]{1,0:T(8,128)S(1)} %get-tuple-element.52), channel_id=1, source_target_pairs={{0,13},{1,112},{4,1},{5,116},{8,5},{9,120},{12,9},{13,124},{16,29}... | collective-permute-start | bytes 393224 | tf_op jit(solution)/shard_map/ppermute | solution.py:64
  (9 other events, 77.3 us)
